TPU v7x, 32 devices: a 4x4x1 block of a 4x4x8 slice. The times are simulated.
32 devices in a mesh: dp: 1 (over z), row: 4 (over y), col: 8 (over x, core).
Axes of the slice: x: 4, y: 4, z: 1, core: 2. Of those that a mesh axis runs over, the one named last changes fastest.
The devices are a block of a 4x4x8 slice.
Arguments:
- pair_rep: bfloat16 [512, 512, 64], P(('dp', 'row'), 'col')
- res_mask: int32 [512], P('dp')
- ln_gamma: float32 [64], replicated
- ln_beta: float32 [64], replicated
- w_q: bfloat16 [64, 64], replicated
- w_k: bfloat16 [64, 64], replicated
- w_v: bfloat16 [64, 64], replicated
- w_b: bfloat16 [64, 4], replicated
- w_g: bfloat16 [64, 64], replicated
- w_o: bfloat16 [64, 64], replicated
Outputs:
- output: bfloat16 [512, 512, 64], P(('dp', 'row'), 'col')
All inputs are finite; a program needn't handle non-finite values.
Results may differ from a plain program's by a relative error of at most 0.00763293.
Values are sent between devices in bfloat16 or wider.
A program may use at most 768 MiB of HBM per device.

v0:
```python
import jax
import jax.numpy as jnp
from jax import lax
from jax.sharding import PartitionSpec as P, NamedSharding

LN_EPS = 1e-5


def layer_norm(pair_rep, ln_gamma, ln_beta):
    pair_f32 = pair_rep.astype(jnp.float32)
    mean_c = jnp.mean(pair_f32, axis=-1, keepdims=True)
    centered = pair_f32 - mean_c
    var_c = jnp.mean(jnp.square(centered), axis=-1, keepdims=True)
    return (centered * lax.rsqrt(var_c + LN_EPS) * ln_gamma + ln_beta).astype(jnp.bfloat16)


def solution(mesh):
    col_size = mesh.shape['col']
    shift_pairs = [(src_dev, (src_dev + 1) % col_size) for src_dev in range(col_size)]
    tile_spec = P(('dp', 'row'), 'col', None)

    def per_device(pair_tile, res_mask, ln_gamma, ln_beta, w_q, w_k, w_v, w_b, w_g, w_o):
        row_len, col_len, chan_dim = pair_tile.shape
        num_heads = w_b.shape[1]
        head_dim = w_q.shape[1] // num_heads
        col_idx = lax.axis_index('col')
        normed = layer_norm(pair_tile, ln_gamma, ln_beta)
        head_shape = (row_len, col_len, num_heads, head_dim)
        queries = (jnp.dot(normed, w_q, preferred_element_type=jnp.float32) * head_dim ** -0.5).astype(jnp.bfloat16).reshape(head_shape)
        key_blk = jnp.dot(normed, w_k, preferred_element_type=jnp.float32).astype(jnp.bfloat16).reshape(head_shape)
        val_blk = jnp.dot(normed, w_v, preferred_element_type=jnp.float32).astype(jnp.bfloat16).reshape(head_shape)
        gate_vals = jax.nn.sigmoid(jnp.dot(normed, w_g, preferred_element_type=jnp.float32))
        bias_tile = jnp.dot(normed, w_b, preferred_element_type=jnp.float32).astype(jnp.bfloat16)
        bias_cols = lax.all_gather(bias_tile, 'row', axis=0, tiled=True)
        bias_rows = lax.all_to_all(bias_cols, 'col', 0, 1, tiled=True)
        key_bias = jnp.where(res_mask > 0, 0.0, -1e9).astype(jnp.float32)
        full_bias = jnp.transpose(bias_rows, (2, 0, 1)).astype(jnp.float32) + key_bias

        def fold_block(fold_state, key_part, val_part, src_col):
            run_max, run_sum, acc_out = fold_state
            bias_part = lax.dynamic_slice_in_dim(full_bias, src_col * col_len, col_len, axis=2)
            logits = jnp.einsum('ijhd,ikhd->ihjk', queries, key_part, preferred_element_type=jnp.float32) + bias_part
            new_max = jnp.maximum(run_max, jnp.max(logits, axis=-1))
            rescale = jnp.exp(run_max - new_max)
            weights = jnp.exp(logits - new_max[..., None])
            run_sum = run_sum * rescale + jnp.sum(weights, axis=-1)
            acc_out = acc_out * rescale[..., None] + jnp.einsum('ihjk,ikhd->ihjd', weights.astype(jnp.bfloat16), val_part, preferred_element_type=jnp.float32)
            return new_max, run_sum, acc_out

        stat_shape = (row_len, num_heads, col_len)
        init_state = (jnp.full(stat_shape, -jnp.inf, jnp.float32), jnp.zeros(stat_shape, jnp.float32), jnp.zeros(stat_shape + (head_dim,), jnp.float32))
        first_state = fold_block(init_state, key_blk, val_blk, col_idx)

        def hop_step(hop_idx, loop_state):
            kv_blocks, fold_state = loop_state
            kv_blocks = lax.ppermute(kv_blocks, 'col', shift_pairs)
            src_col = (col_idx + col_size - hop_idx) % col_size
            return kv_blocks, fold_block(fold_state, kv_blocks[0], kv_blocks[1], src_col)

        final_state = lax.fori_loop(1, col_size, hop_step, ((key_blk, val_blk), first_state))
        run_sum = final_state[1][1]
        acc_out = final_state[1][2]
        attended = jnp.transpose(acc_out / run_sum[..., None], (0, 2, 1, 3)).reshape(row_len, col_len, num_heads * head_dim)
        gated_out = (gate_vals * attended).astype(jnp.bfloat16)
        update = jnp.dot(gated_out, w_o, preferred_element_type=jnp.float32)
        return (pair_tile.astype(jnp.float32) + update).astype(jnp.bfloat16)

    return jax.shard_map(per_device, mesh=mesh, in_specs=(tile_spec, P('dp'), P(), P(), P(), P(), P(), P(), P(), P()), out_specs=tile_spec, check_vma=False)
```

profile of v0, /device:TPU:96, one launch (start us, length us, event | category | flops | bytes accessed | tf_op | source)
XLA Modules:
  0.0 528.8 jit_solution(9838034345494149983)
XLA Ops:
  3.2 1.8 fusion.19
  5.3 12.4 %all_gather.3 = bf16[512,64,4]{0,2,1:T(4,128)(2,1)S(1)} all-gather(bf16[128,64,4]{0,2,1:T(4,128)(2,1)S(1)} %convolution_convert_fusion.2), channel_id=1, replica_groups=mesh['dp'=1,'row'=4,'col'=8] {'row'}, dimensions={0}, use_global_device_ids=true | all-gather | bytes 327680 | tf_op jit(solution)/shard_map/all_gather | solution.py:34
  19.2 4.6 all-to-all-start
  26.3 4.5 copy.47
  30.8 4.5 copy.48
  35.3 4.9 copy.52
  41.3 2.1 convert_bitcast_fusion
  43.5 2.6 copy.50
  48.4 11.4 %add_reduce_fusion.1 = (f32[128,4,64]{2,1,0:T(4,128)S(1)}, f32[128,4,64,64]{2,3,1,0:T(8,128)}) fusion(f32[4,64,64]{1,2,0:T(8,128)S(1)} %dynamic-slice_bitcast_fusion, bf16[128,64,4,16]{1,3,2,0:T(8,128)(2,1)} %copy.47, bf16[128,64,4,16]{1,3,2,0:T(8,128)(2,1)} %copy.48), kind=kOutput, calls=%fused_computation.12 | convolution fusion | flops 71270400 | bytes 10682368 | tf_op jit(solution)/shard_map/ijhd,ikhd->ihjk/dot_general | solution.py:42
  59.8 11.6 %fusion.9 = f32[128,4,64]{2,1,0:T(4,128)} fusion(f32[128,4,64,64]{2,3,1,0:T(8,128)} %get-tuple-element.283, f32[128,4,64]{2,1,0:T(4,128)S(1)} %get-tuple-element.354, f32[4,64,64]{1,2,0:T(8,128)S(1)} %dynamic-slice_bitcast_fusion), kind=kLoop, calls=%fused_computation.14 | loop fusion | flops 6258688 | bytes 8716288 | tf_op jit(solution)/shard_map/reduce_sum | solution.py:46
  71.4 1.8 exponential_multiply_fusion
  73.2 10.4 %broadcast_add_fusion = f32[128,4,64,16]{2,3,1,0:T(8,128)} fusion(f32[128,4,64]{2,1,0:T(4,128)S(1)} %get-tuple-element.280, bf16[128,64,4,16]{1,3,2,0:T(8,128)(2,1)S(1)} %copy.52, f32[128,4,64,64]{2,3,1,0:T(8,128)} %get-tuple-element.283, f32[128,4,64]{2,1,0:T(4,128)S(1)} %get-tuple-element.354, f32[4,64,64]{1,2,0:T(8,128)S(1)} %dynamic-slice_bitcast_fusion), kind=kOutput, calls=%fused_computation.31 | convolution fusion | flops 73924608 | bytes 11862016 | tf_op jit(solution)/shard_map/ihjk,ikhd->ihjd/dot_general | solution.py:47
  83.6 432.3 %while.23 = (s32[]{:T(128)}, bf16[128,64,4,16]{0,3,2,1:T(8,128)(2,1)S(1)}, bf16[128,64,4,16]{0,3,2,1:T(8,128)(2,1)}, f32[128,4,64]{2,1,0:T(4,128)S(1)}, f32[128,...) while((s32[]{:T(128)}, ...), condition=%wide.region_7.8_spmd, body=%wide.region_4.7_spmd.sunk | while | flops 152109072 | bytes 53281244 | solution.py:60
  86.9 12.4 %collective-permute-done = bf16[128,64,4,16]{0,3,2,1:T(8,128)(2,1)S(1)} collective-permute-done((bf16[128,64,4,16]{0,3,2,1:T(8,128)(2,1)S(1)}, bf16[128,64,4,16]{0,3,2,1:T(8,128)(2,1)S(1)}, u32[]{:S(2)}, u32[]{:S(2)}) %collective-permute-start) | collective-permute-done | bytes 1048608 | tf_op jit(solution)/shard_map/while/body/eval_jaxpr/ppermute | solution.py:56
  99.3 3.5 copy.70
  102.8 10.8 %add_reduce_fusion.3 = (f32[128,4,64]{2,1,0:T(4,128)S(1)}, f32[128,4,64,64]{2,3,1,0:T(8,128)}) fusion(f32[4,64,64]{1,2,0:T(8,128)S(1)} %constant_dynamic-slice_fusion.2, bf16[128,64,4,16]{1,3,2,0:T(8,128)(2,1)} %get-tuple-element.387, bf16[128,64,4,16]{1,3,2,0:T(8,128)(2,1)S(1)} %copy.70), kind=kOutput, calls=%fused_computation.1.clone.1 | convolution fusion | flops 71270400 | bytes 10682368 | tf_op jit(solution)/shard_map/while/body/eval_jaxpr/ijhd,ikhd->ihjk/dot_general | solution.py:42
  113.7 10.9 %fusion.52 = f32[128,4,64]{2,1,0:T(4,128)S(1)} fusion(f32[128,4,64,64]{2,3,1,0:T(8,128)} %get-tuple-element.348, f32[128,4,64]{2,1,0:T(4,128)S(1)} %max.11, f32[4,64,64]{1,2,0:T(8,128)S(1)} %constant_dynamic-slice_fusion.2), kind=kLoop, calls=%fused_computation.3.clone.1 | loop fusion | flops 6258688 | bytes 8716288 | tf_op jit(solution)/shard_map/while/body/eval_jaxpr/reduce_sum | solution.py:46
  126.3 4.7 copy.71
  131.0 11.9 %multiply_add_fusion.5 = f32[128,4,64,16]{2,3,1,0:T(8,128)} fusion(f32[128,4,64,16]{2,3,1,0:T(8,128)} %get-tuple-element.371, f32[128,4,64]{2,1,0:T(4,128)} %bitcast.76, bf16[128,64,4,16]{1,3,2,0:T(8,128)(2,1)S(1)} %copy.71, f32[128,4,64,64]{2,3,1,0:T(8,128)} %get-tuple-element.348, f32[128,4,64]{2,1,0:T(4,128)S(1)} %max.11, ...), kind=kOutput, calls=%fused_computation.7.clone.1 | convolution fusion | flops 74448896 | bytes 13959168 | tf_op jit(solution)/shard_map/while/body/eval_jaxpr/ihjk,ikhd->ihjd/dot_general | solution.py:47
  142.9 2.4 copy.86
  147.4 13.6 %collective-permute-done = bf16[128,64,4,16]{0,3,2,1:T(8,128)(2,1)S(1)} collective-permute-done((bf16[128,64,4,16]{0,3,2,1:T(8,128)(2,1)S(1)}, bf16[128,64,4,16]{0,3,2,1:T(8,128)(2,1)S(1)}, u32[]{:S(2)}, u32[]{:S(2)}) %collective-permute-start) | collective-permute-done | bytes 1048608 | tf_op jit(solution)/shard_map/while/body/eval_jaxpr/ppermute | solution.py:56
  161.0 3.5 copy.70
  164.5 10.8 %add_reduce_fusion.3 = (f32[128,4,64]{2,1,0:T(4,128)S(1)}, f32[128,4,64,64]{2,3,1,0:T(8,128)}) fusion(f32[4,64,64]{1,2,0:T(8,128)S(1)} %constant_dynamic-slice_fusion.2, bf16[128,64,4,16]{1,3,2,0:T(8,128)(2,1)} %get-tuple-element.387, bf16[128,64,4,16]{1,3,2,0:T(8,128)(2,1)S(1)} %copy.70), kind=kOutput, calls=%fused_computation.1.clone.1 | convolution fusion | flops 71270400 | bytes 10682368 | tf_op jit(solution)/shard_map/while/body/eval_jaxpr/ijhd,ikhd->ihjk/dot_general | solution.py:42
  175.4 10.9 %fusion.52 = f32[128,4,64]{2,1,0:T(4,128)S(1)} fusion(f32[128,4,64,64]{2,3,1,0:T(8,128)} %get-tuple-element.348, f32[128,4,64]{2,1,0:T(4,128)S(1)} %max.11, f32[4,64,64]{1,2,0:T(8,128)S(1)} %constant_dynamic-slice_fusion.2), kind=kLoop, calls=%fused_computation.3.clone.1 | loop fusion | flops 6258688 | bytes 8716288 | tf_op jit(solution)/shard_map/while/body/eval_jaxpr/reduce_sum | solution.py:46
  188.0 4.7 copy.71
  192.7 11.9 %multiply_add_fusion.5 = f32[128,4,64,16]{2,3,1,0:T(8,128)} fusion(f32[128,4,64,16]{2,3,1,0:T(8,128)} %get-tuple-element.371, f32[128,4,64]{2,1,0:T(4,128)} %bitcast.76, bf16[128,64,4,16]{1,3,2,0:T(8,128)(2,1)S(1)} %copy.71, f32[128,4,64,64]{2,3,1,0:T(8,128)} %get-tuple-element.348, f32[128,4,64]{2,1,0:T(4,128)S(1)} %max.11, ...), kind=kOutput, calls=%fused_computation.7.clone.1 | convolution fusion | flops 74448896 | bytes 13959168 | tf_op jit(solution)/shard_map/while/body/eval_jaxpr/ihjk,ikhd->ihjd/dot_general | solution.py:47
  204.6 2.4 copy.86
  208.3 14.4 %collective-permute-done = bf16[128,64,4,16]{0,3,2,1:T(8,128)(2,1)S(1)} collective-permute-done((bf16[128,64,4,16]{0,3,2,1:T(8,128)(2,1)S(1)}, bf16[128,64,4,16]{0,3,2,1:T(8,128)(2,1)S(1)}, u32[]{:S(2)}, u32[]{:S(2)}) %collective-permute-start) | collective-permute-done | bytes 1048608 | tf_op jit(solution)/shard_map/while/body/eval_jaxpr/ppermute | solution.py:56
  222.7 3.5 copy.70
  226.2 10.8 %add_reduce_fusion.3 = (f32[128,4,64]{2,1,0:T(4,128)S(1)}, f32[128,4,64,64]{2,3,1,0:T(8,128)}) fusion(f32[4,64,64]{1,2,0:T(8,128)S(1)} %constant_dynamic-slice_fusion.2, bf16[128,64,4,16]{1,3,2,0:T(8,128)(2,1)} %get-tuple-element.387, bf16[128,64,4,16]{1,3,2,0:T(8,128)(2,1)S(1)} %copy.70), kind=kOutput, calls=%fused_computation.1.clone.1 | convolution fusion | flops 71270400 | bytes 10682368 | tf_op jit(solution)/shard_map/while/body/eval_jaxpr/ijhd,ikhd->ihjk/dot_general | solution.py:42
  237.1 10.9 %fusion.52 = f32[128,4,64]{2,1,0:T(4,128)S(1)} fusion(f32[128,4,64,64]{2,3,1,0:T(8,128)} %get-tuple-element.348, f32[128,4,64]{2,1,0:T(4,128)S(1)} %max.11, f32[4,64,64]{1,2,0:T(8,128)S(1)} %constant_dynamic-slice_fusion.2), kind=kLoop, calls=%fused_computation.3.clone.1 | loop fusion | flops 6258688 | bytes 8716288 | tf_op jit(solution)/shard_map/while/body/eval_jaxpr/reduce_sum | solution.py:46
  249.6 4.7 copy.71
  254.4 11.9 %multiply_add_fusion.5 = f32[128,4,64,16]{2,3,1,0:T(8,128)} fusion(f32[128,4,64,16]{2,3,1,0:T(8,128)} %get-tuple-element.371, f32[128,4,64]{2,1,0:T(4,128)} %bitcast.76, bf16[128,64,4,16]{1,3,2,0:T(8,128)(2,1)S(1)} %copy.71, f32[128,4,64,64]{2,3,1,0:T(8,128)} %get-tuple-element.348, f32[128,4,64]{2,1,0:T(4,128)S(1)} %max.11, ...), kind=kOutput, calls=%fused_computation.7.clone.1 | convolution fusion | flops 74448896 | bytes 13959168 | tf_op jit(solution)/shard_map/while/body/eval_jaxpr/ihjk,ikhd->ihjd/dot_general | solution.py:47
  266.3 2.4 copy.86
  270.0 14.4 %collective-permute-done = bf16[128,64,4,16]{0,3,2,1:T(8,128)(2,1)S(1)} collective-permute-done((bf16[128,64,4,16]{0,3,2,1:T(8,128)(2,1)S(1)}, bf16[128,64,4,16]{0,3,2,1:T(8,128)(2,1)S(1)}, u32[]{:S(2)}, u32[]{:S(2)}) %collective-permute-start) | collective-permute-done | bytes 1048608 | tf_op jit(solution)/shard_map/while/body/eval_jaxpr/ppermute | solution.py:56
  284.4 3.5 copy.70
  287.9 10.8 %add_reduce_fusion.3 = (f32[128,4,64]{2,1,0:T(4,128)S(1)}, f32[128,4,64,64]{2,3,1,0:T(8,128)}) fusion(f32[4,64,64]{1,2,0:T(8,128)S(1)} %constant_dynamic-slice_fusion.2, bf16[128,64,4,16]{1,3,2,0:T(8,128)(2,1)} %get-tuple-element.387, bf16[128,64,4,16]{1,3,2,0:T(8,128)(2,1)S(1)} %copy.70), kind=kOutput, calls=%fused_computation.1.clone.1 | convolution fusion | flops 71270400 | bytes 10682368 | tf_op jit(solution)/shard_map/while/body/eval_jaxpr/ijhd,ikhd->ihjk/dot_general | solution.py:42
  298.8 10.9 %fusion.52 = f32[128,4,64]{2,1,0:T(4,128)S(1)} fusion(f32[128,4,64,64]{2,3,1,0:T(8,128)} %get-tuple-element.348, f32[128,4,64]{2,1,0:T(4,128)S(1)} %max.11, f32[4,64,64]{1,2,0:T(8,128)S(1)} %constant_dynamic-slice_fusion.2), kind=kLoop, calls=%fused_computation.3.clone.1 | loop fusion | flops 6258688 | bytes 8716288 | tf_op jit(solution)/shard_map/while/body/eval_jaxpr/reduce_sum | solution.py:46
  311.3 4.7 copy.71
  316.1 11.9 %multiply_add_fusion.5 = f32[128,4,64,16]{2,3,1,0:T(8,128)} fusion(f32[128,4,64,16]{2,3,1,0:T(8,128)} %get-tuple-element.371, f32[128,4,64]{2,1,0:T(4,128)} %bitcast.76, bf16[128,64,4,16]{1,3,2,0:T(8,128)(2,1)S(1)} %copy.71, f32[128,4,64,64]{2,3,1,0:T(8,128)} %get-tuple-element.348, f32[128,4,64]{2,1,0:T(4,128)S(1)} %max.11, ...), kind=kOutput, calls=%fused_computation.7.clone.1 | convolution fusion | flops 74448896 | bytes 13959168 | tf_op jit(solution)/shard_map/while/body/eval_jaxpr/ihjk,ikhd->ihjd/dot_general | solution.py:47
  328.0 2.4 copy.86
  331.7 14.4 %collective-permute-done = bf16[128,64,4,16]{0,3,2,1:T(8,128)(2,1)S(1)} collective-permute-done((bf16[128,64,4,16]{0,3,2,1:T(8,128)(2,1)S(1)}, bf16[128,64,4,16]{0,3,2,1:T(8,128)(2,1)S(1)}, u32[]{:S(2)}, u32[]{:S(2)}) %collective-permute-start) | collective-permute-done | bytes 1048608 | tf_op jit(solution)/shard_map/while/body/eval_jaxpr/ppermute | solution.py:56
  346.1 3.5 copy.70
  349.6 10.8 %add_reduce_fusion.3 = (f32[128,4,64]{2,1,0:T(4,128)S(1)}, f32[128,4,64,64]{2,3,1,0:T(8,128)}) fusion(f32[4,64,64]{1,2,0:T(8,128)S(1)} %constant_dynamic-slice_fusion.2, bf16[128,64,4,16]{1,3,2,0:T(8,128)(2,1)} %get-tuple-element.387, bf16[128,64,4,16]{1,3,2,0:T(8,128)(2,1)S(1)} %copy.70), kind=kOutput, calls=%fused_computation.1.clone.1 | convolution fusion | flops 71270400 | bytes 10682368 | tf_op jit(solution)/shard_map/while/body/eval_jaxpr/ijhd,ikhd->ihjk/dot_general | solution.py:42
  360.5 10.9 %fusion.52 = f32[128,4,64]{2,1,0:T(4,128)S(1)} fusion(f32[128,4,64,64]{2,3,1,0:T(8,128)} %get-tuple-element.348, f32[128,4,64]{2,1,0:T(4,128)S(1)} %max.11, f32[4,64,64]{1,2,0:T(8,128)S(1)} %constant_dynamic-slice_fusion.2), kind=kLoop, calls=%fused_computation.3.clone.1 | loop fusion | flops 6258688 | bytes 8716288 | tf_op jit(solution)/shard_map/while/body/eval_jaxpr/reduce_sum | solution.py:46
  373.0 4.7 copy.71
  377.8 11.9 %multiply_add_fusion.5 = f32[128,4,64,16]{2,3,1,0:T(8,128)} fusion(f32[128,4,64,16]{2,3,1,0:T(8,128)} %get-tuple-element.371, f32[128,4,64]{2,1,0:T(4,128)} %bitcast.76, bf16[128,64,4,16]{1,3,2,0:T(8,128)(2,1)S(1)} %copy.71, f32[128,4,64,64]{2,3,1,0:T(8,128)} %get-tuple-element.348, f32[128,4,64]{2,1,0:T(4,128)S(1)} %max.11, ...), kind=kOutput, calls=%fused_computation.7.clone.1 | convolution fusion | flops 74448896 | bytes 13959168 | tf_op jit(solution)/shard_map/while/body/eval_jaxpr/ihjk,ikhd->ihjd/dot_general | solution.py:47
  389.7 2.4 copy.86
  393.4 14.4 %collective-permute-done = bf16[128,64,4,16]{0,3,2,1:T(8,128)(2,1)S(1)} collective-permute-done((bf16[128,64,4,16]{0,3,2,1:T(8,128)(2,1)S(1)}, bf16[128,64,4,16]{0,3,2,1:T(8,128)(2,1)S(1)}, u32[]{:S(2)}, u32[]{:S(2)}) %collective-permute-start) | collective-permute-done | bytes 1048608 | tf_op jit(solution)/shard_map/while/body/eval_jaxpr/ppermute | solution.py:56
  407.8 3.5 copy.70
  411.3 10.8 %add_reduce_fusion.3 = (f32[128,4,64]{2,1,0:T(4,128)S(1)}, f32[128,4,64,64]{2,3,1,0:T(8,128)}) fusion(f32[4,64,64]{1,2,0:T(8,128)S(1)} %constant_dynamic-slice_fusion.2, bf16[128,64,4,16]{1,3,2,0:T(8,128)(2,1)} %get-tuple-element.387, bf16[128,64,4,16]{1,3,2,0:T(8,128)(2,1)S(1)} %copy.70), kind=kOutput, calls=%fused_computation.1.clone.1 | convolution fusion | flops 71270400 | bytes 10682368 | tf_op jit(solution)/shard_map/while/body/eval_jaxpr/ijhd,ikhd->ihjk/dot_general | solution.py:42
  422.1 10.9 %fusion.52 = f32[128,4,64]{2,1,0:T(4,128)S(1)} fusion(f32[128,4,64,64]{2,3,1,0:T(8,128)} %get-tuple-element.348, f32[128,4,64]{2,1,0:T(4,128)S(1)} %max.11, f32[4,64,64]{1,2,0:T(8,128)S(1)} %constant_dynamic-slice_fusion.2), kind=kLoop, calls=%fused_computation.3.clone.1 | loop fusion | flops 6258688 | bytes 8716288 | tf_op jit(solution)/shard_map/while/body/eval_jaxpr/reduce_sum | solution.py:46
  434.7 4.7 copy.71
  439.5 11.9 %multiply_add_fusion.5 = f32[128,4,64,16]{2,3,1,0:T(8,128)} fusion(f32[128,4,64,16]{2,3,1,0:T(8,128)} %get-tuple-element.371, f32[128,4,64]{2,1,0:T(4,128)} %bitcast.76, bf16[128,64,4,16]{1,3,2,0:T(8,128)(2,1)S(1)} %copy.71, f32[128,4,64,64]{2,3,1,0:T(8,128)} %get-tuple-element.348, f32[128,4,64]{2,1,0:T(4,128)S(1)} %max.11, ...), kind=kOutput, calls=%fused_computation.7.clone.1 | convolution fusion | flops 74448896 | bytes 13959168 | tf_op jit(solution)/shard_map/while/body/eval_jaxpr/ihjk,ikhd->ihjd/dot_general | solution.py:47
  451.3 2.4 copy.86
  455.1 14.4 %collective-permute-done = bf16[128,64,4,16]{0,3,2,1:T(8,128)(2,1)S(1)} collective-permute-done((bf16[128,64,4,16]{0,3,2,1:T(8,128)(2,1)S(1)}, bf16[128,64,4,16]{0,3,2,1:T(8,128)(2,1)S(1)}, u32[]{:S(2)}, u32[]{:S(2)}) %collective-permute-start) | collective-permute-done | bytes 1048608 | tf_op jit(solution)/shard_map/while/body/eval_jaxpr/ppermute | solution.py:56
  469.5 3.5 copy.70
  473.0 10.8 %add_reduce_fusion.3 = (f32[128,4,64]{2,1,0:T(4,128)S(1)}, f32[128,4,64,64]{2,3,1,0:T(8,128)}) fusion(f32[4,64,64]{1,2,0:T(8,128)S(1)} %constant_dynamic-slice_fusion.2, bf16[128,64,4,16]{1,3,2,0:T(8,128)(2,1)} %get-tuple-element.387, bf16[128,64,4,16]{1,3,2,0:T(8,128)(2,1)S(1)} %copy.70), kind=kOutput, calls=%fused_computation.1.clone.1 | convolution fusion | flops 71270400 | bytes 10682368 | tf_op jit(solution)/shard_map/while/body/eval_jaxpr/ijhd,ikhd->ihjk/dot_general | solution.py:42
  483.8 10.9 %fusion.52 = f32[128,4,64]{2,1,0:T(4,128)S(1)} fusion(f32[128,4,64,64]{2,3,1,0:T(8,128)} %get-tuple-element.348, f32[128,4,64]{2,1,0:T(4,128)S(1)} %max.11, f32[4,64,64]{1,2,0:T(8,128)S(1)} %constant_dynamic-slice_fusion.2), kind=kLoop, calls=%fused_computation.3.clone.1 | loop fusion | flops 6258688 | bytes 8716288 | tf_op jit(solution)/shard_map/while/body/eval_jaxpr/reduce_sum | solution.py:46
  496.4 4.7 copy.71
  501.1 11.9 %multiply_add_fusion.5 = f32[128,4,64,16]{2,3,1,0:T(8,128)} fusion(f32[128,4,64,16]{2,3,1,0:T(8,128)} %get-tuple-element.371, f32[128,4,64]{2,1,0:T(4,128)} %bitcast.76, bf16[128,64,4,16]{1,3,2,0:T(8,128)(2,1)S(1)} %copy.71, f32[128,4,64,64]{2,3,1,0:T(8,128)} %get-tuple-element.348, f32[128,4,64]{2,1,0:T(4,128)S(1)} %max.11, ...), kind=kOutput, calls=%fused_computation.7.clone.1 | convolution fusion | flops 74448896 | bytes 13959168 | tf_op jit(solution)/shard_map/while/body/eval_jaxpr/ihjk,ikhd->ihjd/dot_general | solution.py:47
  513.0 2.4 copy.86
  515.9 5.1 divide_bitcast_fusion
  521.0 4.6 copy.54
  (139 shorter events, 37.3 us)
Async XLA Ops:
  0.0 23.8 %copy-start = (bf16[64,64]{1,0:T(8,128)(2,1)S(1)}, bf16[64,64]{1,0:T(8,128)(2,1)}, u32[]{:S(2)}) copy-start(bf16[64,64]{1,0:T(8,128)(2,1)} %param.16) | copy-start | bytes 24580
  0.0 5.0 copy-start.13
  3.2 21.1 %copy-start.9 = (bf16[64,64]{1,0:T(8,128)(2,1)S(1)}, bf16[64,64]{1,0:T(8,128)(2,1)}, u32[]{:S(2)}) copy-start(bf16[64,64]{1,0:T(8,128)(2,1)} %param.18) | copy-start | bytes 24580
  5.0 21.2 %copy-start.3 = (bf16[128,64,64]{0,2,1:T(8,128)(2,1)}, bf16[128,64,64]{0,2,1:T(8,128)(2,1)S(1)}, u32[]{:S(2)}) copy-start(bf16[128,64,64]{0,2,1:T(8,128)(2,1)S(1)} %fusion.19) | copy-start | bytes 3145732
  5.1 20.7 %copy-start.10 = (bf16[64,64]{1,0:T(8,128)(2,1)S(1)}, bf16[64,64]{1,0:T(8,128)(2,1)}, u32[]{:S(2)}) copy-start(bf16[64,64]{1,0:T(8,128)(2,1)} %param.17) | copy-start | bytes 24580
  19.2 21.0 %all-to-all-start = ((bf16[8,2,8192]{2,1,0:T(2,128)(2,1)}), bf16[8,2,8192]{2,1,0:T(2,128)(2,1)S(1)}, u32[]{:S(2)}, u32[]{:S(2)}) async-start(bf16[8,2,8192]{2,1,0:T(2,128)(2,1)} %reshape.53), calls=%async_computation | async-start | bytes 524288 | tf_op jit(solution)/shard_map/all_to_all | solution.py:35
  26.2 13.9 %copy-start.12 = (s32[512]{0:T(512)S(1)}, s32[512]{0:T(512)}, u32[]{:S(2)}) copy-start(s32[512]{0:T(512)} %param.13) | copy-start | bytes 6148
  47.4 1.0 copy-start.8
  83.8 15.5 %collective-permute-start = (bf16[128,64,4,16]{0,3,2,1:T(8,128)(2,1)S(1)}, bf16[128,64,4,16]{0,3,2,1:T(8,128)(2,1)S(1)}, u32[]{:S(2)}, u32[]{:S(2)}) collective-permute-start(bf16[128,64,4,16]{0,3,2,1:T(8,128)(2,1)S(1)} %get-tuple-element.367), channel_id=1, source_target_pairs={{0,1},{1,2},{2,3},{3,4},{4,5},{5,6},{6,7},{7,0},{8,9},{9,10},{10,1... | collective-permute-start | bytes 3145736 | tf_op jit(solution)/shard_map/while/body/eval_jaxpr/ppermute | solution.py:56
  84.4 41.9 %collective-permute-start.1 = (bf16[128,64,4,16]{0,3,2,1:T(8,128)(2,1)}, bf16[128,64,4,16]{0,3,2,1:T(8,128)(2,1)}, u32[]{:S(2)}, u32[]{:S(2)}) collective-permute-start(bf16[128,64,4,16]{0,3,2,1:T(8,128)(2,1)} %get-tuple-element.368), channel_id=1, source_target_pairs={{0,1},{1,2},{2,3},{3,4},{4,5},{5,6},{6,7},{7,0},{8,9},{9,10},{10,1... | collective-permute-start | bytes 3145736 | tf_op jit(solution)/shard_map/while/body/eval_jaxpr/ppermute | solution.py:56
  113.7 10.9 %copy-start.6 = (f32[128,4,64]{2,1,0:T(4,128)S(1)}, f32[128,4,64]{2,1,0:T(4,128)}, u32[]{:S(2)}) copy-start(f32[128,4,64]{2,1,0:T(4,128)} %get-tuple-element.370) | copy-start | bytes 393220 | tf_op jit(solution)/shard_map/while
  125.5 0.8 copy-start.7
  142.9 2.6 copy-start.2
  145.5 15.5 %collective-permute-start = (bf16[128,64,4,16]{0,3,2,1:T(8,128)(2,1)S(1)}, bf16[128,64,4,16]{0,3,2,1:T(8,128)(2,1)S(1)}, u32[]{:S(2)}, u32[]{:S(2)}) collective-permute-start(bf16[128,64,4,16]{0,3,2,1:T(8,128)(2,1)S(1)} %get-tuple-element.367), channel_id=1, source_target_pairs={{0,1},{1,2},{2,3},{3,4},{4,5},{5,6},{6,7},{7,0},{8,9},{9,10},{10,1... | collective-permute-start | bytes 3145736 | tf_op jit(solution)/shard_map/while/body/eval_jaxpr/ppermute | solution.py:56
  145.6 42.4 %collective-permute-start.1 = (bf16[128,64,4,16]{0,3,2,1:T(8,128)(2,1)}, bf16[128,64,4,16]{0,3,2,1:T(8,128)(2,1)}, u32[]{:S(2)}, u32[]{:S(2)}) collective-permute-start(bf16[128,64,4,16]{0,3,2,1:T(8,128)(2,1)} %get-tuple-element.368), channel_id=1, source_target_pairs={{0,1},{1,2},{2,3},{3,4},{4,5},{5,6},{6,7},{7,0},{8,9},{9,10},{10,1... | collective-permute-start | bytes 3145736 | tf_op jit(solution)/shard_map/while/body/eval_jaxpr/ppermute | solution.py:56
  175.4 10.9 %copy-start.6 = (f32[128,4,64]{2,1,0:T(4,128)S(1)}, f32[128,4,64]{2,1,0:T(4,128)}, u32[]{:S(2)}) copy-start(f32[128,4,64]{2,1,0:T(4,128)} %get-tuple-element.370) | copy-start | bytes 393220 | tf_op jit(solution)/shard_map/while
  187.2 0.8 copy-start.7
  204.6 2.6 copy-start.2
  207.2 15.5 %collective-permute-start = (bf16[128,64,4,16]{0,3,2,1:T(8,128)(2,1)S(1)}, bf16[128,64,4,16]{0,3,2,1:T(8,128)(2,1)S(1)}, u32[]{:S(2)}, u32[]{:S(2)}) collective-permute-start(bf16[128,64,4,16]{0,3,2,1:T(8,128)(2,1)S(1)} %get-tuple-element.367), channel_id=1, source_target_pairs={{0,1},{1,2},{2,3},{3,4},{4,5},{5,6},{6,7},{7,0},{8,9},{9,10},{10,1... | collective-permute-start | bytes 3145736 | tf_op jit(solution)/shard_map/while/body/eval_jaxpr/ppermute | solution.py:56
  207.3 42.4 %collective-permute-start.1 = (bf16[128,64,4,16]{0,3,2,1:T(8,128)(2,1)}, bf16[128,64,4,16]{0,3,2,1:T(8,128)(2,1)}, u32[]{:S(2)}, u32[]{:S(2)}) collective-permute-start(bf16[128,64,4,16]{0,3,2,1:T(8,128)(2,1)} %get-tuple-element.368), channel_id=1, source_target_pairs={{0,1},{1,2},{2,3},{3,4},{4,5},{5,6},{6,7},{7,0},{8,9},{9,10},{10,1... | collective-permute-start | bytes 3145736 | tf_op jit(solution)/shard_map/while/body/eval_jaxpr/ppermute | solution.py:56
  237.1 10.9 %copy-start.6 = (f32[128,4,64]{2,1,0:T(4,128)S(1)}, f32[128,4,64]{2,1,0:T(4,128)}, u32[]{:S(2)}) copy-start(f32[128,4,64]{2,1,0:T(4,128)} %get-tuple-element.370) | copy-start | bytes 393220 | tf_op jit(solution)/shard_map/while
  248.8 0.8 copy-start.7
  266.3 2.6 copy-start.2
  268.9 15.5 %collective-permute-start = (bf16[128,64,4,16]{0,3,2,1:T(8,128)(2,1)S(1)}, bf16[128,64,4,16]{0,3,2,1:T(8,128)(2,1)S(1)}, u32[]{:S(2)}, u32[]{:S(2)}) collective-permute-start(bf16[128,64,4,16]{0,3,2,1:T(8,128)(2,1)S(1)} %get-tuple-element.367), channel_id=1, source_target_pairs={{0,1},{1,2},{2,3},{3,4},{4,5},{5,6},{6,7},{7,0},{8,9},{9,10},{10,1... | collective-permute-start | bytes 3145736 | tf_op jit(solution)/shard_map/while/body/eval_jaxpr/ppermute | solution.py:56
  269.0 42.4 %collective-permute-start.1 = (bf16[128,64,4,16]{0,3,2,1:T(8,128)(2,1)}, bf16[128,64,4,16]{0,3,2,1:T(8,128)(2,1)}, u32[]{:S(2)}, u32[]{:S(2)}) collective-permute-start(bf16[128,64,4,16]{0,3,2,1:T(8,128)(2,1)} %get-tuple-element.368), channel_id=1, source_target_pairs={{0,1},{1,2},{2,3},{3,4},{4,5},{5,6},{6,7},{7,0},{8,9},{9,10},{10,1... | collective-permute-start | bytes 3145736 | tf_op jit(solution)/shard_map/while/body/eval_jaxpr/ppermute | solution.py:56
  298.7 10.9 %copy-start.6 = (f32[128,4,64]{2,1,0:T(4,128)S(1)}, f32[128,4,64]{2,1,0:T(4,128)}, u32[]{:S(2)}) copy-start(f32[128,4,64]{2,1,0:T(4,128)} %get-tuple-element.370) | copy-start | bytes 393220 | tf_op jit(solution)/shard_map/while
  310.5 0.8 copy-start.7
  328.0 2.6 copy-start.2
  330.6 15.5 %collective-permute-start = (bf16[128,64,4,16]{0,3,2,1:T(8,128)(2,1)S(1)}, bf16[128,64,4,16]{0,3,2,1:T(8,128)(2,1)S(1)}, u32[]{:S(2)}, u32[]{:S(2)}) collective-permute-start(bf16[128,64,4,16]{0,3,2,1:T(8,128)(2,1)S(1)} %get-tuple-element.367), channel_id=1, source_target_pairs={{0,1},{1,2},{2,3},{3,4},{4,5},{5,6},{6,7},{7,0},{8,9},{9,10},{10,1... | collective-permute-start | bytes 3145736 | tf_op jit(solution)/shard_map/while/body/eval_jaxpr/ppermute | solution.py:56
  330.7 42.4 %collective-permute-start.1 = (bf16[128,64,4,16]{0,3,2,1:T(8,128)(2,1)}, bf16[128,64,4,16]{0,3,2,1:T(8,128)(2,1)}, u32[]{:S(2)}, u32[]{:S(2)}) collective-permute-start(bf16[128,64,4,16]{0,3,2,1:T(8,128)(2,1)} %get-tuple-element.368), channel_id=1, source_target_pairs={{0,1},{1,2},{2,3},{3,4},{4,5},{5,6},{6,7},{7,0},{8,9},{9,10},{10,1... | collective-permute-start | bytes 3145736 | tf_op jit(solution)/shard_map/while/body/eval_jaxpr/ppermute | solution.py:56
  360.4 10.9 %copy-start.6 = (f32[128,4,64]{2,1,0:T(4,128)S(1)}, f32[128,4,64]{2,1,0:T(4,128)}, u32[]{:S(2)}) copy-start(f32[128,4,64]{2,1,0:T(4,128)} %get-tuple-element.370) | copy-start | bytes 393220 | tf_op jit(solution)/shard_map/while
  372.2 0.8 copy-start.7
  389.6 2.6 copy-start.2
  392.3 15.5 %collective-permute-start = (bf16[128,64,4,16]{0,3,2,1:T(8,128)(2,1)S(1)}, bf16[128,64,4,16]{0,3,2,1:T(8,128)(2,1)S(1)}, u32[]{:S(2)}, u32[]{:S(2)}) collective-permute-start(bf16[128,64,4,16]{0,3,2,1:T(8,128)(2,1)S(1)} %get-tuple-element.367), channel_id=1, source_target_pairs={{0,1},{1,2},{2,3},{3,4},{4,5},{5,6},{6,7},{7,0},{8,9},{9,10},{10,1... | collective-permute-start | bytes 3145736 | tf_op jit(solution)/shard_map/while/body/eval_jaxpr/ppermute | solution.py:56
  392.4 42.4 %collective-permute-start.1 = (bf16[128,64,4,16]{0,3,2,1:T(8,128)(2,1)}, bf16[128,64,4,16]{0,3,2,1:T(8,128)(2,1)}, u32[]{:S(2)}, u32[]{:S(2)}) collective-permute-start(bf16[128,64,4,16]{0,3,2,1:T(8,128)(2,1)} %get-tuple-element.368), channel_id=1, source_target_pairs={{0,1},{1,2},{2,3},{3,4},{4,5},{5,6},{6,7},{7,0},{8,9},{9,10},{10,1... | collective-permute-start | bytes 3145736 | tf_op jit(solution)/shard_map/while/body/eval_jaxpr/ppermute | solution.py:56
  422.1 10.9 %copy-start.6 = (f32[128,4,64]{2,1,0:T(4,128)S(1)}, f32[128,4,64]{2,1,0:T(4,128)}, u32[]{:S(2)}) copy-start(f32[128,4,64]{2,1,0:T(4,128)} %get-tuple-element.370) | copy-start | bytes 393220 | tf_op jit(solution)/shard_map/while
  433.9 0.8 copy-start.7
  451.3 2.6 copy-start.2
  454.0 15.5 %collective-permute-start = (bf16[128,64,4,16]{0,3,2,1:T(8,128)(2,1)S(1)}, bf16[128,64,4,16]{0,3,2,1:T(8,128)(2,1)S(1)}, u32[]{:S(2)}, u32[]{:S(2)}) collective-permute-start(bf16[128,64,4,16]{0,3,2,1:T(8,128)(2,1)S(1)} %get-tuple-element.367), channel_id=1, source_target_pairs={{0,1},{1,2},{2,3},{3,4},{4,5},{5,6},{6,7},{7,0},{8,9},{9,10},{10,1... | collective-permute-start | bytes 3145736 | tf_op jit(solution)/shard_map/while/body/eval_jaxpr/ppermute | solution.py:56
  454.1 42.4 %collective-permute-start.1 = (bf16[128,64,4,16]{0,3,2,1:T(8,128)(2,1)}, bf16[128,64,4,16]{0,3,2,1:T(8,128)(2,1)}, u32[]{:S(2)}, u32[]{:S(2)}) collective-permute-start(bf16[128,64,4,16]{0,3,2,1:T(8,128)(2,1)} %get-tuple-element.368), channel_id=1, source_target_pairs={{0,1},{1,2},{2,3},{3,4},{4,5},{5,6},{6,7},{7,0},{8,9},{9,10},{10,1... | collective-permute-start | bytes 3145736 | tf_op jit(solution)/shard_map/while/body/eval_jaxpr/ppermute | solution.py:56
  483.8 10.9 %copy-start.6 = (f32[128,4,64]{2,1,0:T(4,128)S(1)}, f32[128,4,64]{2,1,0:T(4,128)}, u32[]{:S(2)}) copy-start(f32[128,4,64]{2,1,0:T(4,128)} %get-tuple-element.370) | copy-start | bytes 393220 | tf_op jit(solution)/shard_map/while
  495.6 0.8 copy-start.7
  513.0 2.6 copy-start.2
  521.0 4.6 copy-start.4
  521.0 4.6 copy-start.14
  521.0 7.3 %copy-start.1 = (bf16[64,64]{1,0:T(8,128)(2,1)S(1)}, bf16[64,64]{1,0:T(8,128)(2,1)}, u32[]{:S(2)}) copy-start(bf16[64,64]{1,0:T(8,128)(2,1)} %param.16) | copy-start | bytes 24580
  525.7 1.2 copy-start.5
  525.7 1.2 copy-start.11
where the time goes:
time: 536 us; the launch traced here: 529 us
  matrix products  186 us (35%)
  local copies, waits for them, and re-layouts  113 us (21%)
  other arithmetic  110 us (21%)
  waiting for transfers between devices  97.9 us (18%)
  blocking collectives  12.4 us (2%)
  starting transfers between devices  8.36 us (2%)
    ppermute x14, waiting for transfers between devices, hop_step(): kv_blocks = lax.ppermute(kv_blocks, 'col', shift_pairs)  97.9 us
    dot_general x8, matrix products, fold_block(): jnp.einsum('ihjk,ikhd->ihjd', weights.astype(jnp.bfloat16), val_part, pre...  93.7 us
    reduce_sum x8, other arithmetic, fold_block(): run_sum = run_sum * rescale + jnp.sum(weights, axis=-1)  87.9 us
    dot_general x8, matrix products, fold_block(): jnp.einsum('ijhd,ikhd->ihjk', queries, key_part, preferred_element_type=j...  86.9 us
    ppermute x14, local copies, waits for them, and re-layouts, hop_step(): kv_blocks = lax.ppermute(kv_blocks, 'col', shift_pairs)  57.4 us
    while x63, local copies, waits for them, and re-layouts  23.9 us
    all_gather x1, blocking collectives, per_device(): bias_cols = lax.all_gather(bias_tile, 'row', axis=0, tiled=True)  12.4 us
  transfers between devices with their start and end apart: 15, of which 7 were waited for; matrix products, arithmetic and copies ran while one was open for 40% of the time, Pallas kernels for 0%

commit v1 on v0

v1 whole, which is shorter than its diff:
```python
import functools

import jax
import jax.numpy as jnp
from jax import lax
from jax.experimental import pallas as pl
from jax.experimental.pallas import tpu as pltpu
from jax.sharding import PartitionSpec as P

LN_EPS = 1e-5
F32 = jnp.float32
BF16 = jnp.bfloat16
MESH = pl.DeviceIdType.MESH


def pack_kernel(z_ref, wb_ref, gamma_ref, beta_ref, zt_ref, bias_ref, acc_ref):
    group = pl.program_id(0)
    rows, cols, chan = z_ref.shape
    half = rows // 2
    heads = bias_ref.shape[0]
    normed = []
    for t in range(half):
        pair = jnp.concatenate([z_ref[t], z_ref[t + half]], axis=0).astype(F32)
        zt = pair.T
        zt_ref[0, t] = zt.astype(BF16)
        mean = jnp.mean(zt, axis=0, keepdims=True)
        cen = zt - mean
        var = jnp.mean(cen * cen, axis=0, keepdims=True)
        normed.append((cen * lax.rsqrt(var + LN_EPS) * gamma_ref[...] + beta_ref[...]).astype(BF16))
    stacked = jnp.concatenate(normed, axis=0)
    bias = jnp.dot(wb_ref[...], stacked, preferred_element_type=F32)
    for h in range(heads):
        acc_ref[h, pl.ds(pl.multiple_of(group * half, half), half), :] = bias[h * half:(h + 1) * half]

    @pl.when(group == pl.num_programs(0) - 1)
    def _():
        n_q = acc_ref.shape[1]
        src = lax.broadcasted_iota(jnp.int32, (n_q, 2 * n_q), 0)
        dst = lax.broadcasted_iota(jnp.int32, (n_q, 2 * n_q), 1)
        base = (src // half) * rows + src % half
        sel0 = jnp.where(dst == base, 1.0, 0.0).astype(BF16)
        sel1 = jnp.where(dst == base + half, 1.0, 0.0).astype(BF16)
        for h in range(heads):
            tr = acc_ref[h].T.astype(BF16)
            out = jnp.dot(tr[:cols], sel0, preferred_element_type=F32)
            out = out + jnp.dot(tr[cols:], sel1, preferred_element_type=F32)
            bias_ref[h] = out.astype(BF16)


def unpack_kernel(r_ref, out_ref):
    half = r_ref.shape[1]
    cols = out_ref.shape[1]
    for t in range(half):
        pair = r_ref[0, t].astype(F32).T.astype(BF16)
        out_ref[t] = pair[:cols]
        out_ref[t + half] = pair[cols:]


def project(t, zbuf, w_t, gamma, beta, heads, zr, qz, kr, vr, gr):
    n_src, _, chan, lanes = zbuf.shape
    half = lanes // 2
    n = n_src * half
    hd = chan // heads
    low = lax.broadcasted_iota(jnp.int32, (chan, lanes), 1) < half
    blk = [zbuf[c, t].astype(F32) for c in range(n_src)]
    rows = ([], [])
    for x in range(n_src // 2):
        a, b = blk[2 * x], blk[2 * x + 1]
        rows[0].append(jnp.where(low, a, pltpu.roll(b, half, 1)))
        rows[1].append(jnp.where(low, pltpu.roll(a, half, 1), b))
    for side in range(2):
        r = 2 * t + side
        z = jnp.concatenate(rows[side], axis=1)
        zr[r] = z
        mean = jnp.mean(z, axis=0, keepdims=True)
        cen = z - mean
        var = jnp.mean(cen * cen, axis=0, keepdims=True)
        normed = (cen * lax.rsqrt(var + LN_EPS) * gamma + beta).astype(BF16)
        proj = jnp.dot(w_t, normed, preferred_element_type=F32)
        q_t = (proj[:chan] * hd ** -0.5).astype(BF16)
        for h in range(heads):
            parts = []
            if h > 0:
                parts.append(jnp.zeros((h * hd, n), BF16))
            parts.append(q_t[h * hd:(h + 1) * hd])
            if h < heads - 1:
                parts.append(jnp.zeros(((heads - 1 - h) * hd, n), BF16))
            qz[r * heads + h] = jnp.concatenate(parts, axis=0)
            vr[r * heads + h] = proj[2 * chan + h * hd:2 * chan + (h + 1) * hd].astype(BF16)
            gr[r * heads + h] = jax.nn.sigmoid(proj[3 * chan + h * hd:3 * chan + (h + 1) * hd])
        kr[r] = proj[chan:2 * chan].T.astype(BF16)


KC = 64
TK = 256
TN = 256


def unit(u, n_unit, heads, bias, qz, kr, vr, gr, sref, mref, gat, do_ex=True, do_qk=True):
    n = sref.shape[-1]
    if do_qk:
        nxt = u + 1 if isinstance(u, int) else jnp.minimum(u + 1, n_unit - 1)
        s = jnp.dot(kr[nxt // heads], qz[nxt], preferred_element_type=F32)
    if do_ex:
        v = vr[u]
        g = gr[u]
        outs = []
        for nb in range(n // TN):
            ns = slice(nb * TN, (nb + 1) * TN)
            mb = jnp.broadcast_to(mref[:, ns], (8, TN))
            total = jnp.zeros((8, TN), F32)
            o = None
            for tk in range(n // TK):
                ks = slice(tk * TK, (tk + 1) * TK)
                p = jnp.exp(sref[ks, ns].reshape(TK // 8, 8, TN) - mb[None])
                total = total + jnp.sum(p, axis=0)
                d = jnp.dot(v[:, ks], p.reshape(TK, TN).astype(BF16), preferred_element_type=F32)
                o = d if o is None else o + d
            outs.append((g[:, ns] * (o / jnp.sum(total, axis=0, keepdims=True))).astype(BF16))
        gat[u] = jnp.concatenate(outs, axis=1)
    if do_qk:
        h = nxt % heads
        top = None
        for kc in range(n // KC):
            sl = slice(kc * KC, (kc + 1) * KC)
            sc = s[sl] + bias[h, sl, :]
            sref[sl, :] = sc
            m8 = jnp.max(sc.reshape(KC // 8, 8, n), axis=0)
            top = m8 if top is None else jnp.maximum(top, m8)
        mref[...] = jnp.max(top, axis=0, keepdims=True)


def finish(t, zr, gat, wo_t, heads, obuf):
    n_src, _, chan, lanes = obuf.shape
    half = lanes // 2
    low = lax.broadcasted_iota(jnp.int32, (chan, lanes), 1) < half
    o = []
    for side in range(2):
        r = 2 * t + side
        gated = jnp.concatenate([gat[r * heads + h] for h in range(heads)], axis=0)
        o.append(zr[r] + jnp.dot(wo_t, gated, preferred_element_type=F32))
    for x in range(n_src // 2):
        a = o[0][:, x * lanes:(x + 1) * lanes]
        b = o[1][:, x * lanes:(x + 1) * lanes]
        obuf[2 * x, t] = jnp.where(low, a, pltpu.roll(b, half, 1)).astype(BF16)
        obuf[2 * x + 1, t] = jnp.where(low, pltpu.roll(a, half, 1), b).astype(BF16)


def attn_kernel(n_col, n_row, zt, bt, kb, w_t, wo_t, gamma, beta, res,
                zbuf, ball, bias, zr, qz, kr, vr, gr, sref, mref, gat, obuf,
                b1_send, b1_recv, z_send, z_recv, b2_send, b2_recv, b3_send, b3_recv,
                o_send, o_recv, own_sem):
    col = lax.axis_index('col')
    row = lax.axis_index('row')
    core = lax.rem(col, 2)
    mate = col + 1 - 2 * core
    heads = bt.shape[0]
    hh = heads // 2
    n_pair = zbuf.shape[1]
    cols = bt.shape[1]

    def at_col(d):
        return lax.rem(col + d, n_col)

    def at_row(d):
        return lax.rem(row + d, n_row)

    barrier = pltpu.get_barrier_semaphore()
    for d in range(1, n_col):
        pl.semaphore_signal(barrier, inc=1, device_id={'col': at_col(d)}, device_id_type=MESH)
    for d in range(1, n_row):
        pl.semaphore_signal(barrier, inc=1, device_id={'row': at_row(d)}, device_id_type=MESH)
    pl.semaphore_wait(barrier, n_col + n_row - 2)

    key_rows = pl.ds(pl.multiple_of(col * cols, cols), cols)
    my_heads = pl.ds(core * hh, hh)

    b1 = []
    for d in range(1, n_col):
        peer = at_col(d)
        side = lax.rem(peer, 2)
        b1.append(pltpu.make_async_remote_copy(
            src_ref=bt.at[pl.ds(side * hh, hh)],
            dst_ref=ball.at[row, pl.ds(side * hh, hh), key_rows, :],
            send_sem=b1_send.at[d - 1], recv_sem=b1_recv.at[d - 1],
            device_id={'col': peer}, device_id_type=MESH))
        b1[-1].start()
    zc = []
    for d in range(1, n_col):
        peer = at_col(d)
        zc.append(pltpu.make_async_remote_copy(
            src_ref=zt.at[peer], dst_ref=zbuf.at[col],
            send_sem=z_send.at[d - 1], recv_sem=z_recv.at[d - 1],
            device_id={'col': peer}, device_id_type=MESH))
        zc[-1].start()
    zbuf[col] = zt[col]
    ball[row, my_heads, key_rows, :] = bt[my_heads]

    for c in b1:
        c.wait_recv()
    b2 = []
    for d in range(1, n_row):
        b2.append(pltpu.make_async_remote_copy(
            src_ref=ball.at[row, my_heads], dst_ref=ball.at[row, my_heads],
            send_sem=b2_send.at[d - 1], recv_sem=b2_recv.at[d - 1],
            device_id={'row': at_row(d)}, device_id_type=MESH))
        b2[-1].start()
    b3 = []
    b3.append(pltpu.make_async_remote_copy(
        src_ref=ball.at[row, my_heads], dst_ref=ball.at[row, my_heads],
        send_sem=b3_send.at[0], recv_sem=b3_recv.at[0],
        device_id={'col': mate}, device_id_type=MESH))
    b3[-1].start()

    for c in zc:
        c.wait_recv()
    w = w_t[...]
    ga = gamma[...]
    be = beta[...]

    def project_body(t, carry):
        project(t, zbuf, w, ga, be, heads, zr, qz, kr, vr, gr)
        return carry

    lax.fori_loop(0, n_pair, project_body, 0)

    for d in range(1, n_row):
        b2[d - 1].wait_recv()
        src_row = lax.rem(row + n_row - d, n_row)
        b3.append(pltpu.make_async_remote_copy(
            src_ref=ball.at[src_row, my_heads], dst_ref=ball.at[src_row, my_heads],
            send_sem=b3_send.at[d], recv_sem=b3_recv.at[d],
            device_id={'col': mate}, device_id_type=MESH))
        b3[-1].start()
    for c in b3:
        c.wait_recv()

    strip = ball.shape[-1]
    for r in range(n_row):
        for h in range(heads):
            bias[h, :, r * strip:(r + 1) * strip] = ball[r, h].astype(F32) + kb[...]

    n_unit = n_pair * 2 * heads
    step = functools.partial(unit, n_unit=n_unit, heads=heads, bias=bias, qz=qz, kr=kr, vr=vr,
                             gr=gr, sref=sref, mref=mref, gat=gat)
    wo = wo_t[...]

    def out_copy(d, t):
        peer = at_col(d)
        return pltpu.make_async_remote_copy(
            src_ref=obuf.at[peer, t], dst_ref=res.at[col, t],
            send_sem=o_send.at[d - 1], recv_sem=o_recv.at[d - 1],
            device_id={'col': peer}, device_id_type=MESH)

    step(-1, do_ex=False)

    def pair_body(t, carry):
        def unit_body(i, c):
            step(t * 2 * heads + i)
            return c
        lax.fori_loop(0, 2 * heads, unit_body, 0)
        finish(t, zr, gat, wo, heads, obuf)
        for d in range(1, n_col):
            out_copy(d, t).start()
        return carry

    lax.fori_loop(0, n_pair, pair_body, 0)

    own = pltpu.make_async_copy(obuf.at[col], res.at[col], own_sem)
    own.start()
    for c in b1 + zc + b2 + b3:
        c.wait_send()
    for d in range(1, n_col):
        peer = at_col(d)
        whole = pltpu.make_async_remote_copy(
            src_ref=obuf.at[peer], dst_ref=res.at[col],
            send_sem=o_send.at[d - 1], recv_sem=o_recv.at[d - 1],
            device_id={'col': peer}, device_id_type=MESH)
        whole.wait_send()
        whole.wait_recv()
    own.wait()


def solution(mesh):
    n_col = mesh.shape['col']
    n_row = mesh.shape['row']
    tile_spec = P(('dp', 'row'), 'col', None)
    vmem = pl.BlockSpec(memory_space=pltpu.VMEM)

    def per_device(pair_tile, res_mask, ln_gamma, ln_beta, w_q, w_k, w_v, w_b, w_g, w_o):
        row_len, col_len, chan = pair_tile.shape
        heads = w_b.shape[1]
        hd = chan // heads
        n = res_mask.shape[0]
        own = row_len // n_col
        half = own // 2
        gamma = ln_gamma.reshape(chan, 1)
        beta = ln_beta.reshape(chan, 1)
        eye = jnp.eye(half, dtype=w_b.dtype)
        wb_big = (w_b.T[:, None, None, :] * eye[None, :, :, None]).reshape(heads * half, half * chan)
        w_t = jnp.concatenate([w_q, w_k, w_v, w_g], axis=1).T
        wo_t = w_o.T
        kb = jnp.broadcast_to(jnp.where(res_mask > 0, 0.0, -1e9).astype(F32)[:, None], (n, row_len))

        zt, bt = pl.pallas_call(
            pack_kernel,
            grid=(n_col,),
            in_specs=[pl.BlockSpec((own, col_len, chan), lambda i: (i, 0, 0)), vmem, vmem, vmem],
            out_specs=[pl.BlockSpec((1, half, chan, 2 * col_len), lambda i: (i, 0, 0, 0)),
                       pl.BlockSpec((heads, col_len, row_len), lambda i: (0, 0, 0))],
            out_shape=[jax.ShapeDtypeStruct((n_col, half, chan, 2 * col_len), BF16),
                       jax.ShapeDtypeStruct((heads, col_len, row_len), BF16)],
            scratch_shapes=[pltpu.VMEM((heads, row_len // 2, 2 * col_len), F32)],
            name='pack',
        )(pair_tile, wb_big, gamma, beta)

        dma = pltpu.SemaphoreType.DMA
        res = pl.pallas_call(
            functools.partial(attn_kernel, n_col, n_row),
            in_specs=[vmem] * 7,
            out_specs=pl.BlockSpec(memory_space=pl.ANY),
            out_shape=jax.ShapeDtypeStruct((n_col, half, chan, 2 * col_len), BF16),
            scratch_shapes=[
                pltpu.VMEM((n_col, half, chan, 2 * col_len), BF16),
                pltpu.VMEM((n_row, heads, n, row_len), BF16),
                pltpu.VMEM((heads, n, n), F32),
                pltpu.VMEM((own, chan, n), F32),
                pltpu.VMEM((own * heads, chan, n), BF16),
                pltpu.VMEM((own, n, chan), BF16),
                pltpu.VMEM((own * heads, hd, n), BF16),
                pltpu.VMEM((own * heads, hd, n), F32),
                pltpu.VMEM((n, n), F32),
                pltpu.VMEM((1, n), F32),
                pltpu.VMEM((own * heads, hd, n), BF16),
                pltpu.VMEM((n_col, half, chan, 2 * col_len), BF16),
                dma((n_col - 1,)), dma((n_col - 1,)), dma((n_col - 1,)), dma((n_col - 1,)),
                dma((n_row - 1,)), dma((n_row - 1,)), dma((n_row,)), dma((n_row,)),
                dma((n_col - 1,)), dma((n_col - 1,)), dma,
            ],
            compiler_params=pltpu.CompilerParams(
                collective_id=0, has_side_effects=True, vmem_limit_bytes=48 << 20),
            name='attention',
        )(zt, bt, kb, w_t, wo_t, gamma, beta)

        return pl.pallas_call(
            unpack_kernel,
            grid=(n_col,),
            in_specs=[pl.BlockSpec((1, half, chan, 2 * col_len), lambda i: (i, 0, 0, 0))],
            out_specs=pl.BlockSpec((own, col_len, chan), lambda i: (i, 0, 0)),
            out_shape=jax.ShapeDtypeStruct((row_len, col_len, chan), BF16),
            name='unpack',
        )(res)

    return jax.shard_map(per_device, mesh=mesh,
                         in_specs=(tile_spec, P('dp'), P(), P(), P(), P(), P(), P(), P(), P()),
                         out_specs=tile_spec, check_vma=False)
```

time: 536 us -> 90 us (0.17)
  the two profiles are of different devices: /device:TPU:96 before, /device:TPU:97 now
where the time goes in v1:
time: 90 us; the launch traced here: 89.6 us
  Pallas kernels  73.4 us (82%)
  local copies, waits for them, and re-layouts  15.8 us (18%)
    pallas_call x1, Pallas kernels, per_device(): pl.pallas_call(functools.partial(attn_kernel, n_col, n_row), in_specs=[vm...  60.3 us
    unnamed x30, local copies, waits for them, and re-layouts  8.25 us
    pallas_call x1, Pallas kernels, per_device(): pl.pallas_call(pack_kernel, grid=(n_col,), in_specs=[pl.BlockSpec((own, c...  7.31 us
    pallas_call x1, Pallas kernels, per_device(): pl.pallas_call(unpack_kernel, grid=(n_col,), in_specs=[pl.BlockSpec((1, h...  5.87 us
    pallas_call x1, local copies, waits for them, and re-layouts, per_device(): pl.pallas_call(unpack_kernel, grid=(n_col,), in_specs=[pl.BlockSpec((1, h...  4.02 us

profile of v1, /device:TPU:97, one launch (start us, length us, event | category | flops | bytes accessed | tf_op | source)
XLA Modules:
  0.0 89.6 jit_solution(17294962709094813048)
XLA Ops:
  0.0 0.0 copy-start.11
  0.0 1.4 %copy.12.gamma_ref.gamma = f32[64,1]{1,0:T(8,128)} copy(f32[64,1]{0,1:T(1,128)} %bitcast.10) | data formatting | bytes 512 | tf_op jit(solution)/shard_map/reshape | solution.py:297
  1.4 1.3 %copy.13.beta_ref.beta = f32[64,1]{1,0:T(8,128)} copy(f32[64,1]{0,1:T(1,128)} %bitcast.11) | data formatting | bytes 512 | tf_op jit(solution)/shard_map/reshape | solution.py:298
  2.7 0.0 copy-start.10
  2.7 4.7 %copy.11.z_ref = bf16[128,64,64]{2,1,0:T(8,128)(2,1)} copy(bf16[128,64,64]{0,2,1:T(8,128)(2,1)} %param.10) | data formatting | bytes 2097152 | tf_op args[0]
  7.5 0.0 copy-start.5
  7.5 0.0 copy-start.6
  7.5 0.0 copy-start.7
  7.5 0.0 copy-start.8
  7.5 0.0 copy-start.9
  7.5 0.0 copy-start.2
  7.5 0.0 copy-start.3
  7.5 0.0 copy-done.11
  7.5 0.1 broadcast_multiply_fusion
  7.6 0.7 mul.20.wb_ref
  8.3 7.3 %pack.1 = (bf16[8,8,64,128]{3,2,1,0:T(8,128)(2,1)}, bf16[4,64,128]{2,1,0:T(8,128)(2,1)}) custom-call(bf16[128,64,64]{2,1,0:T(8,128)(2,1)} %copy.11.z_ref, bf16[32,512]{1,0:T(8,128)(2,1)} %mul.20.wb_ref, f32[64,1]{1,0:T(8,128)} %copy.12.gamma_ref.gamma, f32[64,1]{1,0:T(8,128)} %copy.13.beta_ref.beta), custom_call_target="tpu_custom_call" | custom-call | tf_op jit(solution)/shard_map/pack/pallas_call | solution.py:305
  15.6 0.0 copy-done.10
  15.7 0.1 broadcast_in_dim.18.kb
  15.8 0.0 copy-done.5
  15.8 0.1 copy.14
  15.9 0.0 copy-done.6
  15.9 0.1 copy.15
  16.0 0.0 copy-done.7
  16.0 0.1 copy.16
  16.1 0.0 copy-done.8
  16.1 0.1 copy.17
  16.2 0.0 copy-done.9
  16.2 0.1 copy.18
  16.3 0.0 copy-done.2
  16.3 0.0 copy-done.3
  16.4 0.0 copy-start.1
  16.4 1.2 %copy-done.1 = bf16[8,8,64,128]{3,2,1,0:T(8,128)(2,1)S(1)} copy-done((bf16[8,8,64,128]{3,2,1,0:T(8,128)(2,1)S(1)}, bf16[8,8,64,128]{3,2,1,0:T(8,128)(2,1)}, u32[]{:S(2)}) %copy-start.1) | copy-done | bytes 1048600
  17.6 0.0 copy-start.4
  17.6 0.8 copy-done.4
  18.4 60.3 %attention.1.r_ref = bf16[8,8,64,128]{3,2,1,0:T(8,128)(2,1)S(1)} custom-call(bf16[8,8,64,128]{3,2,1,0:T(8,128)(2,1)S(1)} %copy-done.1, bf16[4,64,128]{2,1,0:T(8,128)(2,1)S(1)} %copy-done.4, f32[512,128]{1,0:T(8,128)S(1)} %broadcast_in_dim.18.kb, bf16[256,64]{1,0:T(8,128)(2,1)S(1)} %maximum_bitcast_fusion.w_t, bf16[64,64]{1,0:T(8,128)(2,1)S(1)} %bitcast.8, ...), custom_call_target="tpu_custom_call" | custom-call | tf_op jit(solution)/shard_map/attention/pallas_call | solution.py:318
  78.7 0.0 copy-start
  78.7 1.0 %copy-done = bf16[8,8,64,128]{3,2,1,0:T(8,128)(2,1)} copy-done((bf16[8,8,64,128]{3,2,1,0:T(8,128)(2,1)}, bf16[8,8,64,128]{3,2,1,0:T(8,128)(2,1)S(1)}, u32[]{:S(2)}) %copy-start) | copy-done | bytes 1048600
  79.7 5.9 %unpack.1 = bf16[128,64,64]{2,1,0:T(8,128)(2,1)} custom-call(bf16[8,8,64,128]{3,2,1,0:T(8,128)(2,1)} %copy-done), custom_call_target="tpu_custom_call" | custom-call | tf_op jit(solution)/shard_map/unpack/pallas_call | solution.py:345
  85.5 4.0 %copy.21 = bf16[128,64,64]{0,2,1:T(8,128)(2,1)} copy(bf16[128,64,64]{2,1,0:T(8,128)(2,1)} %unpack.1) | data formatting | bytes 2097152 | tf_op jit(solution)/shard_map/unpack/pallas_call | solution.py:345
  (3 shorter events, 0.0 us)
Async XLA Ops:
  0.0 7.5 %copy-start.11 = (bf16[64,4]{0,1:T(4,128)(2,1)S(1)}, bf16[64,4]{0,1:T(4,128)(2,1)}, u32[]{:S(2)}) copy-start(bf16[64,4]{0,1:T(4,128)(2,1)} %param.17) | copy-start | bytes 1540
  2.7 12.9 %copy-start.10 = (s32[512]{0:T(512)S(1)}, s32[512]{0:T(512)}, u32[]{:S(2)}) copy-start(s32[512]{0:T(512)} %param.11) | copy-start | bytes 6148
  7.5 8.3 %copy-start.5 = (bf16[64,64]{1,0:T(8,128)(2,1)S(1)}, bf16[64,64]{1,0:T(8,128)(2,1)}, u32[]{:S(2)}) copy-start(bf16[64,64]{1,0:T(8,128)(2,1)} %param.14) | copy-start | bytes 24580
  7.5 8.4 %copy-start.6 = (bf16[64,64]{1,0:T(8,128)(2,1)S(1)}, bf16[64,64]{1,0:T(8,128)(2,1)}, u32[]{:S(2)}) copy-start(bf16[64,64]{1,0:T(8,128)(2,1)} %param.15) | copy-start | bytes 24580
  7.5 8.5 %copy-start.7 = (bf16[64,64]{1,0:T(8,128)(2,1)S(1)}, bf16[64,64]{1,0:T(8,128)(2,1)}, u32[]{:S(2)}) copy-start(bf16[64,64]{1,0:T(8,128)(2,1)} %param.16) | copy-start | bytes 24580
  7.5 8.6 %copy-start.8 = (bf16[64,64]{1,0:T(8,128)(2,1)S(1)}, bf16[64,64]{1,0:T(8,128)(2,1)}, u32[]{:S(2)}) copy-start(bf16[64,64]{1,0:T(8,128)(2,1)} %param.18) | copy-start | bytes 24580
  7.5 8.8 %copy-start.9 = (bf16[64,64]{1,0:T(8,128)(2,1)S(1)}, bf16[64,64]{1,0:T(8,128)(2,1)}, u32[]{:S(2)}) copy-start(bf16[64,64]{1,0:T(8,128)(2,1)} %param.19) | copy-start | bytes 24580
  7.5 8.9 %copy-start.2 = (f32[64,1]{1,0:T(8,128)S(1)}, f32[64,1]{1,0:T(8,128)}, u32[]{:S(2)}) copy-start(f32[64,1]{1,0:T(8,128)} %copy.12.gamma_ref.gamma) | copy-start | bytes 772
  7.5 8.9 %copy-start.3 = (f32[64,1]{1,0:T(8,128)S(1)}, f32[64,1]{1,0:T(8,128)}, u32[]{:S(2)}) copy-start(f32[64,1]{1,0:T(8,128)} %copy.13.beta_ref.beta) | copy-start | bytes 772
  16.4 1.2 %copy-start.1 = (bf16[8,8,64,128]{3,2,1,0:T(8,128)(2,1)S(1)}, bf16[8,8,64,128]{3,2,1,0:T(8,128)(2,1)}, u32[]{:S(2)}) copy-start(bf16[8,8,64,128]{3,2,1,0:T(8,128)(2,1)} %get-tuple-element.7.zt) | copy-start | bytes 3145732
  17.6 0.8 copy-start.4
  78.7 1.0 %copy-start = (bf16[8,8,64,128]{3,2,1,0:T(8,128)(2,1)}, bf16[8,8,64,128]{3,2,1,0:T(8,128)(2,1)S(1)}, u32[]{:S(2)}) copy-start(bf16[8,8,64,128]{3,2,1,0:T(8,128)(2,1)S(1)} %attention.1.r_ref) | copy-start | bytes 3145732

commit v2 on v0

v2 whole, which is shorter than its diff:
```python
import functools

import jax
import jax.numpy as jnp
from jax import lax
from jax.experimental import pallas as pl
from jax.experimental.pallas import tpu as pltpu
from jax.sharding import PartitionSpec as P

LN_EPS = 1e-5
F32 = jnp.float32
BF16 = jnp.bfloat16
MESH = pl.DeviceIdType.MESH

ROWS = 2
KEYS = 64
TILE = 256


def column(row, lanes):
    return jnp.broadcast_to(row, (lanes, row.shape[-1])).T


def layer_norm(z, gamma, beta, axis):
    mean = jnp.mean(z, axis=axis, keepdims=True)
    cen = z - mean
    var = jnp.mean(cen * cen, axis=axis, keepdims=True)
    return (cen * lax.rsqrt(var + LN_EPS) * gamma + beta).astype(BF16)


def tile_bias(zin, wb_t, gamma, beta, bt):
    n_key, chan, n_q = zin.shape
    heads = bt.shape[0]
    group = 16
    wide = jnp.concatenate([wb_t, wb_t], axis=1)
    wide = jnp.concatenate([wide] * (group // 2), axis=1)
    rows = jnp.concatenate([jnp.broadcast_to(wide[h:h + 1], (group, group * chan)) for h in range(heads)], axis=0)
    own = lax.broadcasted_iota(jnp.int32, rows.shape, 0) % group
    src = lax.broadcasted_iota(jnp.int32, rows.shape, 1) // chan
    big = jnp.where(own == src, rows, 0.0).astype(BF16)

    def body(g, carry):
        start = pl.multiple_of(g * group, group)
        normed = layer_norm(zin[pl.ds(start, group)].astype(F32), gamma[None], beta[None], 1)
        out = jnp.dot(big, normed.reshape(group * chan, n_q), preferred_element_type=F32)
        for h in range(heads):
            bt[h, pl.ds(start, group), :] = out[h * group:(h + 1) * group].astype(BF16)
        return carry

    lax.fori_loop(0, n_key // group, body, 0)


def to_rows(zin, zt):
    n_key, chan, _ = zin.shape
    hc = chan // 2
    for s in range(0, hc, 16):
        a = jnp.swapaxes(zin[:, s:s + 16, :].astype(F32), 0, 1)
        b = jnp.swapaxes(zin[:, hc + s:hc + s + 16, :].astype(F32), 0, 1)
        c = jnp.concatenate([a, b], axis=1)
        c = jnp.stack([c[i].T for i in range(16)], axis=0)
        zt[:, s:s + 16, :] = jnp.swapaxes(c, 0, 1).astype(BF16)


def unpack_kernel(r, out):
    n_key, chan, _ = out.shape
    hc = chan // 2
    for s in range(0, hc, 16):
        c = jnp.swapaxes(r[:, s:s + 16, :].astype(F32), 0, 1)
        c = [c[i].T for i in range(16)]
        a = jnp.stack([x[:n_key] for x in c], axis=0)
        b = jnp.stack([x[n_key:] for x in c], axis=0)
        out[:, s:s + 16, :] = jnp.swapaxes(a, 0, 1).astype(BF16)
        out[:, hc + s:hc + s + 16, :] = jnp.swapaxes(b, 0, 1).astype(BF16)


def project(t, zbuf, w_t, gamma, beta, heads, zr, qz, kr, vr, gr):
    n_src, _, hc, lanes = zbuf.shape
    chan = 2 * hc
    half = lanes // 2
    n = n_src * half
    hd = chan // heads
    low = lax.broadcasted_iota(jnp.int32, (hc, lanes), 1) < half
    for side in range(ROWS):
        r = ROWS * t + side
        cols = []
        for x in range(n_src // 2):
            a = zbuf[2 * x, r].astype(F32)
            b = zbuf[2 * x + 1, r].astype(F32)
            top = jnp.where(low, a, pltpu.roll(b, half, 1))
            bot = jnp.where(low, pltpu.roll(a, half, 1), b)
            cols.append(jnp.concatenate([top, bot], axis=0))
        z = jnp.concatenate(cols, axis=1)
        zr[r] = z
        proj = jnp.dot(w_t, layer_norm(z, gamma, beta, 0), preferred_element_type=F32)
        q_t = (proj[:chan] * hd ** -0.5).astype(BF16)
        for h in range(heads):
            parts = []
            if h > 0:
                parts.append(jnp.zeros((h * hd, n), BF16))
            parts.append(q_t[h * hd:(h + 1) * hd])
            if h < heads - 1:
                parts.append(jnp.zeros(((heads - 1 - h) * hd, n), BF16))
            qz[r * heads + h] = jnp.concatenate(parts, axis=0)
            vr[r * heads + h] = proj[2 * chan + h * hd:2 * chan + (h + 1) * hd].astype(BF16)
            gr[r * heads + h] = jax.nn.sigmoid(proj[3 * chan + h * hd:3 * chan + (h + 1) * hd])
        kr[r] = proj[chan:2 * chan].T.astype(BF16)


class Logits:
    def __init__(self, slot, row, head, heads, bias, qz, kr, sref, mref):
        self.slot, self.head, self.bias, self.sref, self.mref = slot, head, bias, sref, mref
        self.value = jnp.dot(kr[row], qz[row * heads + head], preferred_element_type=F32)
        self.top = None
        self.done = 0

    def advance(self):
        n = self.sref.shape[-1]
        if self.done == n:
            return
        sl = slice(self.done, self.done + KEYS)
        self.done += KEYS
        part = self.value[sl] + self.bias[self.head, sl, :]
        self.sref[self.slot, sl, :] = part
        top = jnp.max(part.reshape(KEYS // 8, 8, n), axis=0)
        self.top = top if self.top is None else jnp.maximum(self.top, top)

    def end(self):
        while self.done < self.sref.shape[-1]:
            self.advance()
        self.mref[self.slot] = jnp.max(self.top, axis=0, keepdims=True)


def step(s, n_pair, heads, bias, qz, kr, vr, gr, sref, mref, gat, do_ex=True):
    n = sref.shape[-1]
    hh = heads // 2
    nxt = s + 1 if isinstance(s, int) else jnp.minimum(s + 1, n_pair * hh - 1)

    def place(at, i):
        return (at % n_pair) * ROWS + i // 2, at // n_pair + hh * (i % 2)

    pending = None
    for i in range(2 * ROWS):
        row, head = place(nxt, i)
        logits = Logits(i, row, head, heads, bias, qz, kr, sref, mref)
        if do_ex:
            row, head = place(s, i)
            idx = row * heads + head
            v = vr[idx]
            g = gr[idx]
            outs = []
            for q0 in range(0, n, TILE):
                qs = slice(q0, q0 + TILE)
                peak = jnp.broadcast_to(mref[i, :, qs], (8, TILE))[None]
                total = jnp.zeros((8, TILE), F32)
                acc = None
                for k0 in range(0, n, TILE):
                    parts = []
                    for k1 in range(k0, k0 + TILE, KEYS):
                        p = jnp.exp(sref[i, k1:k1 + KEYS, qs].reshape(KEYS // 8, 8, TILE) - peak)
                        total = total + jnp.sum(p, axis=0)
                        parts.append(p.reshape(KEYS, TILE).astype(BF16))
                        if pending is not None:
                            pending.advance()
                    d = jnp.dot(v[:, k0:k0 + TILE], jnp.concatenate(parts, axis=0), preferred_element_type=F32)
                    acc = d if acc is None else acc + d
                outs.append((g[:, qs] * (acc / jnp.sum(total, axis=0, keepdims=True))).astype(BF16))
            gat[idx] = jnp.concatenate(outs, axis=1)
        if pending is not None:
            pending.end()
        pending = logits
    pending.end()


def finish(t, zr, gat, wo_t, heads, obuf):
    n_src, _, hc, lanes = obuf.shape
    half = lanes // 2
    low = lax.broadcasted_iota(jnp.int32, (hc, lanes), 1) < half
    for side in range(ROWS):
        r = ROWS * t + side
        gated = jnp.concatenate([gat[r * heads + h] for h in range(heads)], axis=0)
        o = zr[r] + jnp.dot(wo_t, gated, preferred_element_type=F32)
        for x in range(n_src // 2):
            top = o[:hc, x * lanes:(x + 1) * lanes]
            bot = o[hc:, x * lanes:(x + 1) * lanes]
            obuf[2 * x, r] = jnp.where(low, top, pltpu.roll(bot, half, 1)).astype(BF16)
            obuf[2 * x + 1, r] = jnp.where(low, pltpu.roll(top, half, 1), bot).astype(BF16)


def attn_kernel(n_col, n_row, zin, mask, gamma_row, beta_row, w_q, w_k, w_v, w_g, wb_t, w_o, res,
                bt, zt, zbuf, ball, bias, kb, zr, qz, kr, vr, gr, sref, mref, gat, obuf,
                b1_send, b1_recv, z_send, z_recv, b2_send, b2_recv, b3_send, b3_recv,
                o_send, o_recv, own_sem):
    col = lax.axis_index('col')
    row = lax.axis_index('row')
    core = lax.rem(col, 2)
    mate = col + 1 - 2 * core
    heads, cols, strip = bt.shape
    hh = heads // 2
    own = zbuf.shape[1]
    n_pair = own // ROWS
    n = sref.shape[-1]

    def at_col(d):
        return lax.rem(col + d, n_col)

    def at_row(d):
        return lax.rem(row + d, n_row)

    def remote(src, dst, send, recv, where):
        return pltpu.make_async_remote_copy(src_ref=src, dst_ref=dst, send_sem=send, recv_sem=recv,
                                            device_id=where, device_id_type=MESH)

    barrier = pltpu.get_barrier_semaphore()
    for d in range(1, n_col):
        pl.semaphore_signal(barrier, inc=1, device_id={'col': at_col(d)}, device_id_type=MESH)
    for d in range(1, n_row):
        pl.semaphore_signal(barrier, inc=1, device_id={'row': at_row(d)}, device_id_type=MESH)

    ga = column(gamma_row[...], strip)
    be = column(beta_row[...], strip)
    tile_bias(zin, wb_t[...].astype(F32), ga, be, bt)
    pl.semaphore_wait(barrier, n_col + n_row - 2)

    key_rows = pl.ds(pl.multiple_of(col * cols, cols), cols)
    my_heads = pl.ds(core * hh, hh)
    b1 = []
    for d in range(1, n_col):
        peer = at_col(d)
        half = pl.ds(lax.rem(peer, 2) * hh, hh)
        b1.append(remote(bt.at[half], ball.at[row, half, key_rows, :],
                         b1_send.at[d - 1], b1_recv.at[d - 1], {'col': peer}))
        b1[-1].start()
    ball[row, my_heads, key_rows, :] = bt[my_heads]

    to_rows(zin, zt)
    part = own // 2
    zc = [[], []]
    for e in range(2):
        for d in range(1, n_col):
            peer = at_col(d)
            zc[e].append(remote(zt.at[pl.ds(peer * own + e * part, part)],
                                zbuf.at[col, pl.ds(e * part, part)],
                                z_send.at[e, d - 1], z_recv.at[e, d - 1], {'col': peer}))
            zc[e][-1].start()
    zbuf[col] = zt[pl.ds(col * own, own)]

    for c in b1:
        c.wait_recv()
    b2 = [[], []]
    b3 = [[], []]
    for e in range(hh):
        head = core * hh + e
        for d in range(1, n_row):
            b2[e].append(remote(ball.at[row, head], ball.at[row, head],
                                b2_send.at[e, d - 1], b2_recv.at[e, d - 1], {'row': at_row(d)}))
            b2[e][-1].start()
        b3[e].append(remote(ball.at[row, head], ball.at[row, head],
                            b3_send.at[e, 0], b3_recv.at[e, 0], {'col': mate}))
        b3[e][-1].start()

    def pass_on(e):
        head = core * hh + e
        for d in range(1, n_row):
            b2[e][d - 1].wait_recv()
            from_row = lax.rem(row + n_row - d, n_row)
            b3[e].append(remote(ball.at[from_row, head], ball.at[from_row, head],
                                b3_send.at[e, d], b3_recv.at[e, d], {'col': mate}))
            b3[e][-1].start()

    def take_bias(e):
        for c in b3[e]:
            c.wait_recv()
        for h in range(e, heads, hh):
            for r in range(n_row):
                bias[h, :, r * strip:(r + 1) * strip] = ball[r, h].astype(F32) + kb[...]

    kb[...] = column(jnp.where(mask[...] > 0, 0.0, -1e9).astype(F32), strip)
    w_t = jnp.concatenate([w[...].astype(F32).T for w in (w_q, w_k, w_v, w_g)], axis=0).astype(BF16)
    wo_t = w_o[...].astype(F32).T.astype(BF16)
    ga_n = jnp.concatenate([ga] * (n // strip), axis=1)
    be_n = jnp.concatenate([be] * (n // strip), axis=1)

    def project_body(t, carry):
        project(t, zbuf, w_t, ga_n, be_n, heads, zr, qz, kr, vr, gr)
        return carry

    for c in zc[0]:
        c.wait_recv()
    lax.fori_loop(0, n_pair // 2, project_body, 0)
    pass_on(0)
    for c in zc[1]:
        c.wait_recv()
    lax.fori_loop(n_pair // 2, n_pair, project_body, 0)
    take_bias(0)

    run = functools.partial(step, n_pair=n_pair, heads=heads, bias=bias, qz=qz, kr=kr, vr=vr,
                            gr=gr, sref=sref, mref=mref, gat=gat)

    def early_body(s, carry):
        run(s)
        return carry

    run(-1, do_ex=False)
    lax.fori_loop(0, n_pair // 2, early_body, 0)
    pass_on(1)
    lax.fori_loop(n_pair // 2, n_pair - 1, early_body, 0)
    take_bias(1)
    run(n_pair - 1)

    def late_body(t, carry):
        run(n_pair + t)
        finish(t, zr, gat, wo_t, heads, obuf)
        rows = pl.ds(ROWS * t, ROWS)
        for d in range(1, n_col):
            peer = at_col(d)
            remote(obuf.at[peer, rows], res.at[col, rows],
                   o_send.at[d - 1], o_recv.at[d - 1], {'col': peer}).start()
        return carry

    lax.fori_loop(0, n_pair, late_body, 0)

    mine = pltpu.make_async_copy(obuf.at[col], res.at[col], own_sem)
    mine.start()
    for c in b1 + zc[0] + zc[1] + b2[0] + b2[1] + b3[0] + b3[1]:
        c.wait_send()
    for d in range(1, n_col):
        peer = at_col(d)
        whole = remote(obuf.at[peer], res.at[col], o_send.at[d - 1], o_recv.at[d - 1], {'col': peer})
        whole.wait_send()
        whole.wait_recv()
    mine.wait()


def solution(mesh):
    n_col = mesh.shape['col']
    n_row = mesh.shape['row']
    tile_spec = P(('dp', 'row'), 'col', None)
    vmem = pl.BlockSpec(memory_space=pltpu.VMEM)

    def per_device(pair_tile, res_mask, ln_gamma, ln_beta, w_q, w_k, w_v, w_b, w_g, w_o):
        row_len, col_len, chan = pair_tile.shape
        heads = w_b.shape[1]
        hd = chan // heads
        n = res_mask.shape[0]
        own = row_len // n_col
        hc = chan // 2
        lanes = 2 * col_len
        dma = pltpu.SemaphoreType.DMA
        res = pl.pallas_call(
            functools.partial(attn_kernel, n_col, n_row),
            in_specs=[vmem] * 10,
            out_specs=pl.BlockSpec(memory_space=pl.ANY),
            out_shape=jax.ShapeDtypeStruct((n_col, own, hc, lanes), BF16),
            scratch_shapes=[
                pltpu.VMEM((heads, col_len, row_len), BF16),
                pltpu.VMEM((row_len, hc, lanes), BF16),
                pltpu.VMEM((n_col, own, hc, lanes), BF16),
                pltpu.VMEM((n_row, heads, n, row_len), BF16),
                pltpu.VMEM((heads, n, n), F32),
                pltpu.VMEM((n, row_len), F32),
                pltpu.VMEM((own, chan, n), F32),
                pltpu.VMEM((own * heads, chan, n), BF16),
                pltpu.VMEM((own, n, chan), BF16),
                pltpu.VMEM((own * heads, hd, n), BF16),
                pltpu.VMEM((own * heads, hd, n), F32),
                pltpu.VMEM((2 * ROWS, n, n), F32),
                pltpu.VMEM((2 * ROWS, 1, n), F32),
                pltpu.VMEM((own * heads, hd, n), BF16),
                pltpu.VMEM((n_col, own, hc, lanes), BF16),
                dma((n_col - 1,)), dma((n_col - 1,)), dma((2, n_col - 1)), dma((2, n_col - 1)),
                dma((heads // 2, n_row - 1)), dma((heads // 2, n_row - 1)),
                dma((heads // 2, n_row)), dma((heads // 2, n_row)),
                dma((n_col - 1,)), dma((n_col - 1,)), dma,
            ],
            compiler_params=pltpu.CompilerParams(
                collective_id=0, has_side_effects=True, vmem_limit_bytes=52 << 20),
            name='attention',
        )(jnp.transpose(pair_tile, (1, 2, 0)), res_mask.reshape(1, n), ln_gamma.reshape(1, chan),
          ln_beta.reshape(1, chan), w_q, w_k, w_v, w_g, w_b.T, w_o)

        out = pl.pallas_call(
            unpack_kernel,
            in_specs=[vmem],
            out_specs=vmem,
            out_shape=jax.ShapeDtypeStruct((col_len, chan, row_len), BF16),
            name='unpack',
        )(res.reshape(row_len, hc, lanes))
        return jnp.transpose(out, (2, 0, 1))

    return jax.shard_map(per_device, mesh=mesh,
                         in_specs=(tile_spec, P('dp'), P(), P(), P(), P(), P(), P(), P(), P()),
                         out_specs=tile_spec, check_vma=False)
```

time: 536 us -> 62 us (0.12)
  the two profiles are of different devices: /device:TPU:96 before, /device:TPU:97 now
where the time goes in v2:
time: 62 us; the launch traced here: 61.5 us
  Pallas kernels  56.2 us (91%)
  local copies, waits for them, and re-layouts  5.24 us (8%)
    pallas_call x1, Pallas kernels, per_device(): pl.pallas_call(functools.partial(attn_kernel, n_col, n_row), in_specs=[vm...  53 us
    unnamed x20, local copies, waits for them, and re-layouts  5.24 us
    pallas_call x1, Pallas kernels, per_device(): pl.pallas_call(unpack_kernel, in_specs=[vmem], out_specs=vmem, out_shape=...  3.18 us

profile of v2, /device:TPU:97, one launch (start us, length us, event | category | flops | bytes accessed | tf_op | source)
XLA Modules:
  0.0 61.5 jit_solution(14291055504286084594)
XLA Ops:
  0.0 0.0 copy-start.9
  0.0 0.0 copy-start.6
  0.0 0.0 copy-start.7
  0.0 0.0 copy-start.8
  0.0 0.6 %copy-done.9 = f32[64]{0:T(128)S(1)} copy-done((f32[64]{0:T(128)S(1)}, f32[64]{0:T(128)}, u32[]{:S(2)}) %copy-start.9) | copy-done | bytes 280
  0.7 0.0 copy-done.6
  0.7 0.0 copy-done.7
  0.7 0.0 copy-done.8
  0.7 0.0 copy-start.1
  0.7 0.7 %copy-done.1 = bf16[64,64]{1,0:T(8,128)(2,1)S(1)} copy-done((bf16[64,64]{1,0:T(8,128)(2,1)S(1)}, bf16[64,64]{1,0:T(8,128)(2,1)}, u32[]{:S(2)}) %copy-start.1) | copy-done | bytes 8216
  1.4 0.0 copy-start.2
  1.4 0.7 %copy-done.2 = bf16[64,64]{1,0:T(8,128)(2,1)S(1)} copy-done((bf16[64,64]{1,0:T(8,128)(2,1)S(1)}, bf16[64,64]{1,0:T(8,128)(2,1)}, u32[]{:S(2)}) %copy-start.2) | copy-done | bytes 8216
  2.2 0.0 copy-start.3
  2.2 0.7 %copy-done.3 = bf16[64,64]{1,0:T(8,128)(2,1)S(1)} copy-done((bf16[64,64]{1,0:T(8,128)(2,1)S(1)}, bf16[64,64]{1,0:T(8,128)(2,1)}, u32[]{:S(2)}) %copy-start.3) | copy-done | bytes 8216
  2.9 0.0 copy-start.4
  2.9 0.7 %copy-done.4 = bf16[64,64]{1,0:T(8,128)(2,1)S(1)} copy-done((bf16[64,64]{1,0:T(8,128)(2,1)S(1)}, bf16[64,64]{1,0:T(8,128)(2,1)}, u32[]{:S(2)}) %copy-start.4) | copy-done | bytes 8216
  3.6 0.0 copy-start.5
  3.6 0.7 %copy-done.5 = bf16[64,64]{1,0:T(8,128)(2,1)S(1)} copy-done((bf16[64,64]{1,0:T(8,128)(2,1)S(1)}, bf16[64,64]{1,0:T(8,128)(2,1)}, u32[]{:S(2)}) %copy-start.5) | copy-done | bytes 8216
  4.3 53.0 %attention.1 = bf16[8,16,32,128]{3,2,1,0:T(8,128)(2,1)S(1)} custom-call(bf16[64,64,128]{2,1,0:T(8,128)(2,1)} %bitcast.12, s32[1,512]{1,0:T(1,128)S(1)} %bitcast.8, f32[1,64]{1,0:T(1,128)S(1)} %bitcast.10, f32[1,64]{1,0:T(1,128)S(1)} %bitcast.11, bf16[64,64]{1,0:T(8,128)(2,1)S(1)} %copy-done.1, bf16[64,64]{1,0:T(8,128)(2,1)S(1)} %copy-done.2, ...), custom_call_target="tpu_custom_call" | custom-call | tf_op jit(solution)/shard_map/attention/pallas_call | solution.py:349
  57.3 0.0 copy-start
  57.3 1.0 %copy-done = bf16[8,16,32,128]{3,2,1,0:T(8,128)(2,1)} copy-done((bf16[8,16,32,128]{3,2,1,0:T(8,128)(2,1)}, bf16[8,16,32,128]{3,2,1,0:T(8,128)(2,1)S(1)}, u32[]{:S(2)}) %copy-start) | copy-done | bytes 1048600
  58.3 3.2 %unpack.1 = bf16[64,64,128]{2,1,0:T(8,128)(2,1)} custom-call(bf16[128,32,128]{2,1,0:T(8,128)(2,1)} %bitcast.7), custom_call_target="tpu_custom_call" | custom-call | tf_op jit(solution)/shard_map/unpack/pallas_call | solution.py:381
Async XLA Ops:
  0.0 0.7 %copy-start.9 = (f32[64]{0:T(128)S(1)}, f32[64]{0:T(128)}, u32[]{:S(2)}) copy-start(f32[64]{0:T(128)} %param.13) | copy-start | bytes 772
  0.0 0.7 %copy-start.6 = (s32[512]{0:T(512)S(1)}, s32[512]{0:T(512)}, u32[]{:S(2)}) copy-start(s32[512]{0:T(512)} %param.11) | copy-start | bytes 6148
  0.0 0.7 %copy-start.7 = (bf16[64,4]{0,1:T(4,128)(2,1)S(1)}, bf16[64,4]{0,1:T(4,128)(2,1)}, u32[]{:S(2)}) copy-start(bf16[64,4]{0,1:T(4,128)(2,1)} %param.17) | copy-start | bytes 1540
  0.0 0.7 %copy-start.8 = (f32[64]{0:T(128)S(1)}, f32[64]{0:T(128)}, u32[]{:S(2)}) copy-start(f32[64]{0:T(128)} %param.12) | copy-start | bytes 772
  0.7 0.7 %copy-start.1 = (bf16[64,64]{1,0:T(8,128)(2,1)S(1)}, bf16[64,64]{1,0:T(8,128)(2,1)}, u32[]{:S(2)}) copy-start(bf16[64,64]{1,0:T(8,128)(2,1)} %w_q.1) | copy-start | bytes 24580
  1.4 0.7 %copy-start.2 = (bf16[64,64]{1,0:T(8,128)(2,1)S(1)}, bf16[64,64]{1,0:T(8,128)(2,1)}, u32[]{:S(2)}) copy-start(bf16[64,64]{1,0:T(8,128)(2,1)} %w_k.1) | copy-start | bytes 24580
  2.2 0.7 %copy-start.3 = (bf16[64,64]{1,0:T(8,128)(2,1)S(1)}, bf16[64,64]{1,0:T(8,128)(2,1)}, u32[]{:S(2)}) copy-start(bf16[64,64]{1,0:T(8,128)(2,1)} %w_v.1) | copy-start | bytes 24580
  2.9 0.7 %copy-start.4 = (bf16[64,64]{1,0:T(8,128)(2,1)S(1)}, bf16[64,64]{1,0:T(8,128)(2,1)}, u32[]{:S(2)}) copy-start(bf16[64,64]{1,0:T(8,128)(2,1)} %w_g.1) | copy-start | bytes 24580
  3.6 0.7 %copy-start.5 = (bf16[64,64]{1,0:T(8,128)(2,1)S(1)}, bf16[64,64]{1,0:T(8,128)(2,1)}, u32[]{:S(2)}) copy-start(bf16[64,64]{1,0:T(8,128)(2,1)} %w_o.1) | copy-start | bytes 24580
  57.3 1.0 %copy-start = (bf16[8,16,32,128]{3,2,1,0:T(8,128)(2,1)}, bf16[8,16,32,128]{3,2,1,0:T(8,128)(2,1)S(1)}, u32[]{:S(2)}) copy-start(bf16[8,16,32,128]{3,2,1,0:T(8,128)(2,1)S(1)} %attention.1) | copy-start | bytes 3145732

commit v3 on v2

v3 whole, which is shorter than its diff:
```python
import functools

import jax
import jax.numpy as jnp
from jax import lax
from jax.experimental import pallas as pl
from jax.experimental.pallas import tpu as pltpu
from jax.sharding import PartitionSpec as P

LN_EPS = 1e-5
F32 = jnp.float32
BF16 = jnp.bfloat16
MESH = pl.DeviceIdType.MESH

KEYS = 64
TILE = 256


def column(row, lanes):
    return jnp.broadcast_to(row, (lanes, row.shape[-1])).T


def layer_norm(z, gamma, beta, axis):
    mean = jnp.mean(z, axis=axis, keepdims=True)
    cen = z - mean
    var = jnp.mean(cen * cen, axis=axis, keepdims=True)
    return (cen * lax.rsqrt(var + LN_EPS) * gamma + beta).astype(BF16)


def tile_bias(zin, wb_t, gamma, beta, bt):
    n_key, chan, n_q = zin.shape
    heads = bt.shape[0]
    group = 16
    wide = jnp.concatenate([wb_t, wb_t], axis=1)
    wide = jnp.concatenate([wide] * (group // 2), axis=1)
    rows = jnp.concatenate([jnp.broadcast_to(wide[h:h + 1], (group, group * chan)) for h in range(heads)], axis=0)
    own = lax.broadcasted_iota(jnp.int32, rows.shape, 0) % group
    src = lax.broadcasted_iota(jnp.int32, rows.shape, 1) // chan
    big = jnp.where(own == src, rows, 0.0).astype(BF16)

    def body(g, carry):
        start = pl.multiple_of(g * group, group)
        normed = layer_norm(zin[pl.ds(start, group)].astype(F32), gamma[None], beta[None], 1)
        out = jnp.dot(big, normed.reshape(group * chan, n_q), preferred_element_type=F32)
        for h in range(heads):
            bt[h, pl.ds(start, group), :] = out[h * group:(h + 1) * group].astype(BF16)
        return carry

    lax.fori_loop(0, n_key // group, body, 0)


def to_rows(zin, zt):
    n_key, chan, _ = zin.shape
    hc = chan // 2
    for s in range(0, hc, 16):
        a = jnp.swapaxes(zin[:, s:s + 16, :].astype(F32), 0, 1)
        b = jnp.swapaxes(zin[:, hc + s:hc + s + 16, :].astype(F32), 0, 1)
        c = jnp.concatenate([a, b], axis=1)
        c = jnp.stack([c[i].T for i in range(16)], axis=0)
        zt[:, s:s + 16, :] = jnp.swapaxes(c, 0, 1).astype(BF16)


def unpack_kernel(r, out):
    n_key = out.shape[0]
    pairs = r.shape[1]
    c = jnp.swapaxes(r[...].astype(F32), 0, 1)
    c = [c[i].T for i in range(pairs)]
    for half in range(2):
        x = jnp.stack([y[half * n_key:(half + 1) * n_key] for y in c], axis=0)
        out[:, half] = jnp.swapaxes(x, 0, 1).astype(BF16)


def project(r, zbuf, w_t, gamma, beta, heads, zr, qz, kr, vr, gr):
    n_src, _, hc, lanes = zbuf.shape
    chan = 2 * hc
    half = lanes // 2
    n = n_src * half
    hd = chan // heads
    low = lax.broadcasted_iota(jnp.int32, (hc, lanes), 1) < half
    cols = []
    for x in range(n_src // 2):
        a = zbuf[2 * x, r].astype(F32)
        b = zbuf[2 * x + 1, r].astype(F32)
        top = jnp.where(low, a, pltpu.roll(b, half, 1))
        bot = jnp.where(low, pltpu.roll(a, half, 1), b)
        cols.append(jnp.concatenate([top, bot], axis=0))
    z = jnp.concatenate(cols, axis=1)
    zr[r] = z
    proj = jnp.dot(w_t, layer_norm(z, gamma, beta, 0), preferred_element_type=F32)
    q_t = (proj[:chan] * hd ** -0.5).astype(BF16)
    for h in range(heads):
        parts = []
        if h > 0:
            parts.append(jnp.zeros((h * hd, n), BF16))
        parts.append(q_t[h * hd:(h + 1) * hd])
        if h < heads - 1:
            parts.append(jnp.zeros(((heads - 1 - h) * hd, n), BF16))
        qz[r * heads + h] = jnp.concatenate(parts, axis=0)
        vr[r * heads + h] = proj[2 * chan + h * hd:2 * chan + (h + 1) * hd].astype(BF16)
        gr[r * heads + h] = jax.nn.sigmoid(proj[3 * chan + h * hd:3 * chan + (h + 1) * hd])
    kr[r] = proj[chan:2 * chan].T.astype(BF16)


class Logits:
    def __init__(self, slot, row, head, heads, bias, qz, kr, sref, mref):
        self.slot, self.head, self.bias, self.sref, self.mref = slot, head, bias, sref, mref
        self.value = jnp.dot(kr[row], qz[row * heads + head], preferred_element_type=F32)
        self.top = None
        self.done = 0

    def advance(self):
        n = self.sref.shape[-1]
        if self.done == n:
            return
        sl = slice(self.done, self.done + KEYS)
        self.done += KEYS
        part = self.value[sl] + self.bias[self.head, sl, :]
        self.sref[self.slot, sl, :] = part
        top = jnp.max(part.reshape(KEYS // 8, 8, n), axis=0)
        self.top = top if self.top is None else jnp.maximum(self.top, top)

    def end(self):
        while self.done < self.sref.shape[-1]:
            self.advance()
        self.mref[self.slot] = jnp.max(self.top, axis=0, keepdims=True)


def step(s, early, own, heads, bias, qz, kr, vr, gr, sref, mref, gat, do_ex=True):
    n = sref.shape[-1]
    hh = heads // 2
    nxt = s + 1 if isinstance(s, int) else jnp.minimum(s + 1, own - 1)

    def place(at, i):
        split = at < 2 * early
        row = jnp.where(split, (at % early) * 2 + i // hh, at)
        head = jnp.where(split, at // early + hh * (i % hh), i)
        return row, head

    pending = None
    for i in range(heads):
        row, head = place(nxt, i)
        logits = Logits(i, row, head, heads, bias, qz, kr, sref, mref)
        if do_ex:
            row, head = place(s, i)
            idx = row * heads + head
            v = vr[idx]
            g = gr[idx]
            outs = []
            for q0 in range(0, n, TILE):
                qs = slice(q0, q0 + TILE)
                peak = jnp.broadcast_to(mref[i, :, qs], (8, TILE))[None]
                total = jnp.zeros((8, TILE), F32)
                acc = None
                for k0 in range(0, n, TILE):
                    parts = []
                    for k1 in range(k0, k0 + TILE, KEYS):
                        p = jnp.exp(sref[i, k1:k1 + KEYS, qs].reshape(KEYS // 8, 8, TILE) - peak)
                        total = total + jnp.sum(p, axis=0)
                        parts.append(p.reshape(KEYS, TILE).astype(BF16))
                        if pending is not None:
                            pending.advance()
                    d = jnp.dot(v[:, k0:k0 + TILE], jnp.concatenate(parts, axis=0), preferred_element_type=F32)
                    acc = d if acc is None else acc + d
                outs.append((g[:, qs] * (acc / jnp.sum(total, axis=0, keepdims=True))).astype(BF16))
            gat[idx] = jnp.concatenate(outs, axis=1)
        if pending is not None:
            pending.end()
        pending = logits
    pending.end()


def finish(r, zr, gat, wo_t, heads, obuf):
    n_src, _, hc, lanes = obuf.shape
    half = lanes // 2
    low = lax.broadcasted_iota(jnp.int32, (hc, lanes), 1) < half
    gated = jnp.concatenate([gat[r * heads + h] for h in range(heads)], axis=0)
    o = zr[r] + jnp.dot(wo_t, gated, preferred_element_type=F32)
    for x in range(n_src // 2):
        top = o[:hc, x * lanes:(x + 1) * lanes]
        bot = o[hc:, x * lanes:(x + 1) * lanes]
        obuf[2 * x, r] = jnp.where(low, top, pltpu.roll(bot, half, 1)).astype(BF16)
        obuf[2 * x + 1, r] = jnp.where(low, pltpu.roll(top, half, 1), bot).astype(BF16)


def attn_kernel(n_col, n_row, zin_h, mask_h, gamma_h, beta_h, wq_h, wk_h, wv_h, wg_h, wb_h, wo_h, res,
                zin, mask, gamma_row, beta_row, w_q, w_k, w_v, w_g, wb_t, w_o,
                bt, zt, zbuf, ball, bias, kb, zr, qz, kr, vr, gr, sref, mref, gat, obuf, w_t, wo_t, affine,
                in_sem, b1_send, b1_recv, z_send, z_recv, b2_send, b2_recv, b3_send, b3_recv,
                o_send, o_recv, own_sem):
    col = lax.axis_index('col')
    row = lax.axis_index('row')
    core = lax.rem(col, 2)
    mate = col + 1 - 2 * core
    heads, cols, strip = bt.shape
    hh = heads // 2
    own = zbuf.shape[1]
    n = sref.shape[-1]
    n_part = z_send.shape[0]
    part = own // n_part
    early = own // 4

    def at_col(d):
        return lax.rem(col + d, n_col)

    def at_row(d):
        return lax.rem(row + d, n_row)

    def remote(src, dst, send, recv, where):
        return pltpu.make_async_remote_copy(src_ref=src, dst_ref=dst, send_sem=send, recv_sem=recv,
                                            device_id=where, device_id_type=MESH)

    loads = [pltpu.make_async_copy(src, dst, in_sem.at[i]) for i, (src, dst) in enumerate((
        (gamma_h, gamma_row), (beta_h, beta_row), (wb_h, wb_t), (zin_h, zin), (mask_h, mask),
        (wq_h, w_q), (wk_h, w_k), (wv_h, w_v), (wg_h, w_g), (wo_h, w_o)))]
    for c in loads:
        c.start()

    barrier = pltpu.get_barrier_semaphore()
    for d in range(1, n_col):
        pl.semaphore_signal(barrier, inc=1, device_id={'col': at_col(d)}, device_id_type=MESH)
    for d in range(1, n_row):
        pl.semaphore_signal(barrier, inc=1, device_id={'row': at_row(d)}, device_id_type=MESH)

    for c in loads[:4]:
        c.wait()
    ga = column(gamma_row[...], strip)
    be = column(beta_row[...], strip)
    tile_bias(zin, wb_t[...].astype(F32), ga, be, bt)
    pl.semaphore_wait(barrier, n_col + n_row - 2)

    def keys_of(c):
        return pl.ds(pl.multiple_of(c * cols, cols), cols)

    def first(e, d):
        peer = at_col(d)
        head = lax.rem(peer, 2) * hh + e
        return remote(bt.at[head], ball.at[row, head, keys_of(col), :],
                      b1_send.at[e, d - 1], b1_recv.at[e, d - 1], {'col': peer})

    def second(e, src, c, d):
        head = core * hh + e
        return remote(src, ball.at[row, head, keys_of(c), :],
                      b2_send.at[e, d - 1], b2_recv.at[e, d - 1], {'row': at_row(d)})

    for e in range(hh):
        for d in range(1, n_col):
            first(e, d).start()
        if e == 0:
            for d in range(1, n_row):
                second(e, bt.at[core * hh + e], col, d).start()

    def rows_out(q, d):
        peer = at_col(d)
        return remote(zt.at[pl.ds(peer * own + q * part, part)], zbuf.at[col, pl.ds(q * part, part)],
                      z_send.at[q, d - 1], z_recv.at[q, d - 1], {'col': peer})

    to_rows(zin, zt)
    for q in range(n_part):
        for d in range(1, n_col):
            rows_out(q, d).start()

    for e in range(hh):
        head = core * hh + e
        if e > 0:
            for d in range(1, n_row):
                second(e, bt.at[head], col, d).start()
        ball[row, head, keys_of(col), :] = bt[head]
        for d in range(1, n_col):
            first(e, d).wait_recv()
            src = lax.rem(col + n_col - d, n_col)
            for f in range(1, n_row):
                second(e, ball.at[row, head, keys_of(src), :], src, f).start()

    def third(e, d):
        head = core * hh + e
        from_row = lax.rem(row + n_row - d, n_row)
        return remote(ball.at[from_row, head], ball.at[from_row, head],
                      b3_send.at[e, d], b3_recv.at[e, d], {'col': mate})

    def whole_second(e, d):
        head = core * hh + e
        return remote(ball.at[row, head], ball.at[row, head],
                      b2_send.at[e, d - 1], b2_recv.at[e, d - 1], {'row': at_row(d)})

    def pass_on(e):
        for d in range(n_row):
            if d > 0:
                whole_second(e, d).wait_recv()
            third(e, d).start()

    def take_bias(e):
        for d in range(n_row):
            third(e, d).wait_recv()
        for h in range(e, heads, hh):
            for r in range(n_row):
                bias[h, :, r * strip:(r + 1) * strip] = ball[r, h].astype(F32) + kb[...]

    for c in loads[4:]:
        c.wait()
    kb[...] = column(jnp.where(mask[...] > 0, 0.0, -1e9).astype(F32), strip)
    w_t[...] = jnp.concatenate([w[...].astype(F32).T for w in (w_q, w_k, w_v, w_g)], axis=0).astype(BF16)
    wo_t[...] = w_o[...].astype(F32).T.astype(BF16)
    affine[0] = ga
    affine[1] = be
    zbuf[col] = zt[pl.ds(col * own, own)]

    def take_rows(q):
        for d in range(1, n_col):
            rows_out(q, d).wait_recv()
        wide = [jnp.concatenate([affine[i]] * (n // strip), axis=1) for i in range(2)]

        def body(r, carry):
            project(r, zbuf, w_t[...], wide[0], wide[1], heads, zr, qz, kr, vr, gr)
            return carry

        lax.fori_loop(q * part, (q + 1) * part, body, 0)

    run = functools.partial(step, early=early, own=own, heads=heads, bias=bias, qz=qz, kr=kr, vr=vr,
                            gr=gr, sref=sref, mref=mref, gat=gat)

    def give_row(r):
        finish(r, zr, gat, wo_t[...], heads, obuf)
        for d in range(1, n_col):
            peer = at_col(d)
            remote(obuf.at[peer, r], res.at[col, r], o_send.at[d - 1], o_recv.at[d - 1], {'col': peer}).start()

    take_rows(0)
    pass_on(0)
    take_bias(0)
    run(-1, do_ex=False)

    def body(s, carry):
        @pl.when(s == 0)
        def _():
            take_rows(1)

        @pl.when(s == 1)
        def _():
            pass_on(1)

        @pl.when(s == early - 2)
        def _():
            take_bias(1)

        @pl.when(s == early)
        def _():
            take_rows(2)

        @pl.when(s == early + 2)
        def _():
            take_rows(3)

        run(s)

        @pl.when((s >= early) & (s < 2 * early))
        def _():
            for i in range(2):
                give_row((s - early) * 2 + i)

        @pl.when(s >= 2 * early)
        def _():
            give_row(s)

        return carry

    lax.fori_loop(0, own, body, 0)

    mine = pltpu.make_async_copy(obuf.at[col], res.at[col], own_sem)
    mine.start()
    for e in range(hh):
        for d in range(1, n_col):
            first(e, d).wait_send()
        for d in range(1, n_row):
            whole_second(e, d).wait_send()
        for d in range(n_row):
            third(e, d).wait_send()
    for q in range(n_part):
        for d in range(1, n_col):
            rows_out(q, d).wait_send()
    for d in range(1, n_col):
        peer = at_col(d)
        whole = remote(obuf.at[peer], res.at[col], o_send.at[d - 1], o_recv.at[d - 1], {'col': peer})
        whole.wait_send()
        whole.wait_recv()
    mine.wait()


def solution(mesh):
    n_col = mesh.shape['col']
    n_row = mesh.shape['row']
    tile_spec = P(('dp', 'row'), 'col', None)
    hbm = pl.BlockSpec(memory_space=pltpu.HBM)
    n_part = 4

    def per_device(pair_tile, res_mask, ln_gamma, ln_beta, w_q, w_k, w_v, w_b, w_g, w_o):
        row_len, col_len, chan = pair_tile.shape
        heads = w_b.shape[1]
        hd = chan // heads
        n = res_mask.shape[0]
        own = row_len // n_col
        hc = chan // 2
        lanes = 2 * col_len
        dma = pltpu.SemaphoreType.DMA
        res = pl.pallas_call(
            functools.partial(attn_kernel, n_col, n_row),
            in_specs=[hbm] * 10,
            out_specs=hbm,
            out_shape=jax.ShapeDtypeStruct((n_col, own, hc, lanes), BF16),
            scratch_shapes=[
                pltpu.VMEM((col_len, chan, row_len), BF16),
                pltpu.VMEM((1, n), res_mask.dtype),
                pltpu.VMEM((1, chan), F32),
                pltpu.VMEM((1, chan), F32),
                pltpu.VMEM(w_q.shape, BF16),
                pltpu.VMEM(w_k.shape, BF16),
                pltpu.VMEM(w_v.shape, BF16),
                pltpu.VMEM(w_g.shape, BF16),
                pltpu.VMEM((heads, chan), BF16),
                pltpu.VMEM(w_o.shape, BF16),
                pltpu.VMEM((heads, col_len, row_len), BF16),
                pltpu.VMEM((row_len, hc, lanes), BF16),
                pltpu.VMEM((n_col, own, hc, lanes), BF16),
                pltpu.VMEM((n_row, heads, n, row_len), BF16),
                pltpu.VMEM((heads, n, n), F32),
                pltpu.VMEM((n, row_len), F32),
                pltpu.VMEM((own, chan, n), F32),
                pltpu.VMEM((own * heads, chan, n), BF16),
                pltpu.VMEM((own, n, chan), BF16),
                pltpu.VMEM((own * heads, hd, n), BF16),
                pltpu.VMEM((own * heads, hd, n), F32),
                pltpu.VMEM((heads, n, n), F32),
                pltpu.VMEM((heads, 1, n), F32),
                pltpu.VMEM((own * heads, hd, n), BF16),
                pltpu.VMEM((n_col, own, hc, lanes), BF16),
                pltpu.VMEM((4 * chan, chan), BF16),
                pltpu.VMEM((chan, chan), BF16),
                pltpu.VMEM((2, chan, row_len), F32),
                dma((10,)),
                dma((heads // 2, n_col - 1)), dma((heads // 2, n_col - 1)),
                dma((n_part, n_col - 1)), dma((n_part, n_col - 1)),
                dma((heads // 2, n_row - 1)), dma((heads // 2, n_row - 1)),
                dma((heads // 2, n_row)), dma((heads // 2, n_row)),
                dma((n_col - 1,)), dma((n_col - 1,)), dma,
            ],
            compiler_params=pltpu.CompilerParams(
                collective_id=0, has_side_effects=True, vmem_limit_bytes=56 << 20),
            name='attention',
        )(jnp.transpose(pair_tile, (1, 2, 0)), res_mask.reshape(1, n), ln_gamma.reshape(1, chan),
          ln_beta.reshape(1, chan), w_q, w_k, w_v, w_g, w_b.T, w_o)

        pairs = 16
        out = pl.pallas_call(
            unpack_kernel,
            grid=(hc // pairs,),
            in_specs=[pl.BlockSpec((row_len, pairs, lanes), lambda i: (0, i, 0))],
            out_specs=pl.BlockSpec((col_len, 2, pairs, row_len), lambda i: (0, 0, i, 0)),
            out_shape=jax.ShapeDtypeStruct((col_len, 2, hc, row_len), BF16),
            name='unpack',
        )(res.reshape(row_len, hc, lanes)).reshape(col_len, chan, row_len)
        return jnp.transpose(out, (2, 0, 1))

    return jax.shard_map(per_device, mesh=mesh,
                         in_specs=(tile_spec, P('dp'), P(), P(), P(), P(), P(), P(), P(), P()),
                         out_specs=tile_spec, check_vma=False)
```

time: 62 us -> 60.3 us (0.973)
  local copies, waits for them, and re-layouts: 5.24 us -> 0 us
  Pallas kernels: 56.2 us -> 60.1 us
    unnamed x20 -> x0, local copies, waits for them, and re-layouts: 5.24 us -> none
    pallas_call x2, Pallas kernels: 56.2 us -> 60.1 us  [the longest x1 57.3 us: per_device(): pl.pallas_call(functools.partial(attn_kernel, n_col, n_row), in_specs=[hb...]
where the time goes in v3:
time: 60.3 us; the launch traced here: 60.2 us
  Pallas kernels  60.1 us (100%)
    pallas_call x1, Pallas kernels, per_device(): pl.pallas_call(functools.partial(attn_kernel, n_col, n_row), in_specs=[hb...  57.3 us
    pallas_call x1, Pallas kernels, per_device(): pl.pallas_call(unpack_kernel, grid=(hc // pairs,), in_specs=[pl.BlockSpec...  2.89 us

profile of v3, /device:TPU:97, one launch (start us, length us, event | category | flops | bytes accessed | tf_op | source)
XLA Modules:
  0.0 60.2 jit_solution(14366500826774322278)
XLA Ops:
  0.0 57.3 %attention.1 = bf16[8,16,32,128]{3,2,1,0:T(8,128)(2,1)} custom-call(bf16[64,64,128]{2,1,0:T(8,128)(2,1)} %bitcast.10, s32[1,512]{1,0:T(1,128)} %bitcast.11, f32[1,64]{1,0:T(1,128)} %bitcast.13, f32[1,64]{1,0:T(1,128)} %bitcast.14, bf16[64,64]{1,0:T(8,128)(2,1)} %wq_h.1, bf16[64,64]{1,0:T(8,128)(2,1)} %wk_h.1, bf16[64,64]{1,0:T(8,128)(2,1)} %wv_h.1, ...), custom_call_target="tpu_custom_call" | custom-call | tf_op jit(solution)/shard_map/attention/pallas_call | solution.py:404
  57.3 2.9 %unpack.1 = bf16[64,2,32,128]{3,2,1,0:T(8,128)(2,1)} custom-call(bf16[128,32,128]{2,1,0:T(8,128)(2,1)} %bitcast.9), custom_call_target="tpu_custom_call" | custom-call | tf_op jit(solution)/shard_map/unpack/pallas_call | solution.py:452

commit v4 on v3

--- a/solution.py
+++ b/solution.py
@@ -125,24 +125,14 @@
         self.mref[self.slot] = jnp.max(self.top, axis=0, keepdims=True)
 
 
-def step(s, early, own, heads, bias, qz, kr, vr, gr, sref, mref, gat, do_ex=True):
+def step(s, own, heads, bias, qz, kr, vr, gr, sref, mref, gat, do_ex=True):
     n = sref.shape[-1]
-    hh = heads // 2
     nxt = s + 1 if isinstance(s, int) else jnp.minimum(s + 1, own - 1)
-
-    def place(at, i):
-        split = at < 2 * early
-        row = jnp.where(split, (at % early) * 2 + i // hh, at)
-        head = jnp.where(split, at // early + hh * (i % hh), i)
-        return row, head
-
     pending = None
     for i in range(heads):
-        row, head = place(nxt, i)
-        logits = Logits(i, row, head, heads, bias, qz, kr, sref, mref)
+        logits = Logits(i, nxt, i, heads, bias, qz, kr, sref, mref)
         if do_ex:
-            row, head = place(s, i)
-            idx = row * heads + head
+            idx = s * heads + i
             v = vr[idx]
             g = gr[idx]
             outs = []
@@ -197,7 +187,6 @@
     n = sref.shape[-1]
     n_part = z_send.shape[0]
     part = own // n_part
-    early = own // 4
 
     def at_col(d):
         return lax.rem(col + d, n_col)
@@ -288,12 +277,9 @@
                 whole_second(e, d).wait_recv()
             third(e, d).start()
 
-    def take_bias(e):
-        for d in range(n_row):
-            third(e, d).wait_recv()
-        for h in range(e, heads, hh):
-            for r in range(n_row):
-                bias[h, :, r * strip:(r + 1) * strip] = ball[r, h].astype(F32) + kb[...]
+    def widen(h):
+        for r in range(n_row):
+            bias[h, :, r * strip:(r + 1) * strip] = ball[r, h].astype(F32) + kb[...]
 
     for c in loads[4:]:
         c.wait()
@@ -315,55 +301,42 @@
 
         lax.fori_loop(q * part, (q + 1) * part, body, 0)
 
-    run = functools.partial(step, early=early, own=own, heads=heads, bias=bias, qz=qz, kr=kr, vr=vr,
+    run = functools.partial(step, own=own, heads=heads, bias=bias, qz=qz, kr=kr, vr=vr,
                             gr=gr, sref=sref, mref=mref, gat=gat)
 
+    def make_row(r):
+        finish(r, zr, gat, wo_t[...], heads, obuf)
+
     def give_row(r):
-        finish(r, zr, gat, wo_t[...], heads, obuf)
         for d in range(1, n_col):
             peer = at_col(d)
             remote(obuf.at[peer, r], res.at[col, r], o_send.at[d - 1], o_recv.at[d - 1], {'col': peer}).start()
 
-    take_rows(0)
-    pass_on(0)
-    take_bias(0)
+    for q in range(n_part):
+        if q == n_part - 1:
+            pass_on(0)
+        take_rows(q)
+    pass_on(1)
+    for e in range(hh):
+        widen(core * hh + e)
+    for e in range(hh):
+        for d in range(n_row):
+            third(e, d).wait_recv()
+    for e in range(hh):
+        widen((1 - core) * hh + e)
+
     run(-1, do_ex=False)
+    run(0)
 
     def body(s, carry):
-        @pl.when(s == 0)
-        def _():
-            take_rows(1)
-
-        @pl.when(s == 1)
-        def _():
-            pass_on(1)
-
-        @pl.when(s == early - 2)
-        def _():
-            take_bias(1)
-
-        @pl.when(s == early)
-        def _():
-            take_rows(2)
-
-        @pl.when(s == early + 2)
-        def _():
-            take_rows(3)
-
+        make_row(s - 1)
         run(s)
-
-        @pl.when((s >= early) & (s < 2 * early))
-        def _():
-            for i in range(2):
-                give_row((s - early) * 2 + i)
-
-        @pl.when(s >= 2 * early)
-        def _():
-            give_row(s)
-
+        give_row(s - 1)
         return carry
 
-    lax.fori_loop(0, own, body, 0)
+    lax.fori_loop(1, own, body, 0)
+    make_row(own - 1)
+    give_row(own - 1)
 
     mine = pltpu.make_async_copy(obuf.at[col], res.at[col], own_sem)
     mine.start()

time: 60.3 us -> 56.1 us (0.930)
  Pallas kernels: 60.1 us -> 55.9 us
    pallas_call x1, Pallas kernels: 57.3 us -> 53.1 us  [per_device(): pl.pallas_call(functools.partial(attn_kernel, n_col, n_row), in_specs=[hb...]
where the time goes in v4:
time: 56.1 us; the launch traced here: 56 us
  Pallas kernels  55.9 us (100%)
    pallas_call x1, Pallas kernels, per_device(): pl.pallas_call(functools.partial(attn_kernel, n_col, n_row), in_specs=[hb...  53.1 us
    pallas_call x1, Pallas kernels, per_device(): pl.pallas_call(unpack_kernel, grid=(hc // pairs,), in_specs=[pl.BlockSpec...  2.89 us

profile of v4, /device:TPU:97, one launch (start us, length us, event | category | flops | bytes accessed | tf_op | source)
XLA Modules:
  0.0 56.0 jit_solution(11291573548033831365)
XLA Ops:
  0.0 53.1 %attention.1 = bf16[8,16,32,128]{3,2,1,0:T(8,128)(2,1)} custom-call(bf16[64,64,128]{2,1,0:T(8,128)(2,1)} %bitcast.10, s32[1,512]{1,0:T(1,128)} %bitcast.11, f32[1,64]{1,0:T(1,128)} %bitcast.13, f32[1,64]{1,0:T(1,128)} %bitcast.14, bf16[64,64]{1,0:T(8,128)(2,1)} %wq_h.1, bf16[64,64]{1,0:T(8,128)(2,1)} %wk_h.1, bf16[64,64]{1,0:T(8,128)(2,1)} %wv_h.1, ...), custom_call_target="tpu_custom_call" | custom-call | tf_op jit(solution)/shard_map/attention/pallas_call | solution.py:377
  53.1 2.9 %unpack.1 = bf16[64,2,32,128]{3,2,1,0:T(8,128)(2,1)} custom-call(bf16[128,32,128]{2,1,0:T(8,128)(2,1)} %bitcast.9), custom_call_target="tpu_custom_call" | custom-call | tf_op jit(solution)/shard_map/unpack/pallas_call | solution.py:425
